TPU v7x, 1024 devices: a whole 8x8x8 slice. The times are simulated.
1024 devices in a mesh: node: 32 (over z_hi, y), dev: 32 (over x, z_lo, core).
Axes of the slice: x: 8, y: 8, z: 8 (z_hi: 4, z_lo: 2; z = z_hi * 2 + z_lo), core: 2. Of those that a mesh axis runs over, the one named last changes fastest.
Arguments:
- tokens: bfloat16 [4096, 5120], P(('node', 'dev')), may hold values from -6 to 6
- node_pick: int32 [4096, 3], P(('node', 'dev')), may hold values from 0 to 31, as said below
- expert_pick: int32 [4096, 6], P(('node', 'dev')), may hold values from 0 to 3, as said below
- gate_weight: bfloat16 [4096, 6], P(('node', 'dev')), may hold values from 0.099609375 to 1
- w_gate: bfloat16 [98304, 5120], P(('node', 'dev')), may hold values from -0.078125 to 0.078125
- w_up: bfloat16 [98304, 5120], P(('node', 'dev')), may hold values from -0.078125 to 0.078125
- w_down: bfloat16 [98304, 5120], P(('node', 'dev')), may hold values from -0.21875 to 0.21875
Outputs:
- mixed_out: bfloat16 [4096, 5120], P(('node', 'dev'))
Inputs may be any that keep to these rules, and one draw needn't show every extreme that they name: `node_pick`: A token's three nodes differ. On every device at most 2 of its 4 tokens choose one node, and some node is chosen by exactly 2 of them. `expert_pick`: columns 2k and 2k + 1 name two different experts of node node_pick[t, k]. Among the tokens of all devices with one index along dev, at most 12 of those choosing one node pick one same expert of it; this is reached somewhere in every draw.
All inputs are finite; a program needn't handle non-finite values.
Results may differ from a plain program's by a relative error of at most 0.009.
Values may be sent and summed in bfloat16 or wider, within the bound.
No kernel may reach another device: no remote copies, remote signals or barrier semaphores. Data moves between devices by JAX's collectives and lax.ppermute only.
A program may use at most 64 MiB of HBM per device.

v0:
```python
import jax
import jax.numpy as jnp
from jax import lax
from jax.experimental import pallas as pl
from jax.experimental.pallas import tpu as pltpu
from jax.sharding import Mesh
from jax.sharding import PartitionSpec as P


EXP_NODE = 4
ALL = ("node", "e", "s")


def swap(a, axis):
    return lax.all_to_all(a, axis, split_axis=0, concat_axis=0, tiled=True)


def cut_kernel(order, gate, up, down, *refs):
    outs, sem = refs[:-1], refs[-1]
    parts = len(outs)
    rows = gate.shape[0]
    width = gate.shape[1] // parts
    copies = []
    for k in range(parts):
        column = pl.multiple_of(order[k] * width, width)
        for i, source in enumerate((gate, up, down)):
            copies.append(
                pltpu.make_async_copy(
                    source.at[:, pl.ds(column, width)],
                    outs[k].at[pl.ds(i * rows, rows), :],
                    sem.at[3 * k + i],
                )
            )
    for copy in copies:
        copy.start()
    for copy in copies:
        copy.wait()


def cut_weights(order, w_gate, w_up, w_down, parts):
    rows, feature_dim = w_gate.shape
    width = feature_dim // parts
    anywhere = pl.BlockSpec(memory_space=pl.ANY)
    return pl.pallas_call(
        cut_kernel,
        in_specs=[pl.BlockSpec(memory_space=pltpu.SMEM)] + [anywhere] * 3,
        out_specs=[anywhere] * parts,
        out_shape=[jax.ShapeDtypeStruct((3 * rows, width), w_gate.dtype)] * parts,
        scratch_shapes=[pltpu.SemaphoreType.DMA((3 * parts,))],
        name="cut_weights",
    )(order, w_gate, w_up, w_down)


def act_kernel(order, rows, *refs):
    blocks, out = refs[:-1], refs[-1]
    weights = jnp.concatenate([block[...] for block in blocks], axis=0)
    made = lax.dot_general(
        weights, rows[...], (((1,), (1,)), ((), ())), preferred_element_type=jnp.float32
    ).astype(jnp.bfloat16)
    size = blocks[0].shape[0]
    for k in range(len(blocks)):
        out[order[k]] = made[k * size : (k + 1) * size]


def partial_acts(order, rows, blocks):
    all_rows, width = rows.shape
    size = blocks[0].shape[0] // 3 * 2
    parts = len(blocks)
    return pl.pallas_call(
        act_kernel,
        grid=(1,),
        in_specs=[
            pl.BlockSpec(memory_space=pltpu.SMEM),
            pl.BlockSpec((all_rows, width), lambda i: (0, 0)),
        ]
        + [pl.BlockSpec((size, width), lambda i: (0, 0))] * parts,
        out_specs=pl.BlockSpec((parts, size, all_rows), lambda i: (0, 0, 0)),
        out_shape=jax.ShapeDtypeStruct((parts, size, all_rows), jnp.bfloat16),
        name="partial_acts",
    )(order, rows, *blocks)


def down_kernel(order, hidden, *refs):
    blocks, out = refs[:-1], refs[-1]
    weights = jnp.concatenate([block[...] for block in blocks], axis=0)
    units = jnp.concatenate([hidden[order[k]] for k in range(len(blocks))], axis=0)
    out[...] = lax.dot_general(
        units, weights, (((0,), (0,)), ((), ())), preferred_element_type=jnp.float32
    ).astype(jnp.bfloat16)


def down_rows(order, hidden, blocks):
    parts, size, all_rows = hidden.shape
    width = blocks[0].shape[1]
    return pl.pallas_call(
        down_kernel,
        grid=(1,),
        in_specs=[
            pl.BlockSpec(memory_space=pltpu.SMEM),
            pl.BlockSpec((parts, size, all_rows), lambda i: (0, 0, 0)),
        ]
        + [pl.BlockSpec((size, width), lambda i: (2, 0))] * parts,
        out_specs=pl.BlockSpec((all_rows, width), lambda i: (0, 0)),
        out_shape=jax.ShapeDtypeStruct((all_rows, width), jnp.bfloat16),
        name="down_rows",
    )(order, hidden, *blocks)


def on_device(tokens, node_pick, expert_pick, gate_weight, w_gate, w_up, w_down):
    node_count = lax.axis_size("node")
    slices = lax.axis_size("s")
    dev_count = EXP_NODE * slices
    tok_rows, feature_dim = tokens.shape
    width = feature_dim // slices
    slot_count = 3 * tok_rows
    cycle_len = min(node_count, max(3, slot_count // 2))
    node_cap = (slot_count + cycle_len - 1) // cycle_len
    node_slots = node_count * node_cap
    hidden_rows = w_gate.shape[0]
    all_rows = dev_count * slot_count

    order = jnp.arange(slices, dtype=jnp.int32) ^ lax.axis_index("s").astype(jnp.int32)
    cut = cut_weights(order, w_gate, w_up, w_down, slices)
    blocks = [cut[0]]
    for k in range(1, slices):
        blocks.append(lax.ppermute(cut[k], "s", [(a, a ^ k) for a in range(slices)]))

    dest_node = node_pick.reshape(slot_count)
    slot_order = jnp.arange(slot_count, dtype=jnp.int32)
    earlier = (dest_node[:, None] == dest_node[None, :]) & (
        slot_order[None, :] < slot_order[:, None]
    )
    slot_rank = jnp.sum(earlier.astype(jnp.int32), axis=1)
    position = dest_node * node_cap + slot_rank
    place = jnp.arange(node_slots, dtype=jnp.int32)[:, None] == position[None, :]
    home = jnp.sum(place.reshape(node_slots, tok_rows, 3).astype(jnp.bfloat16), axis=2)
    local_pick = expert_pick.reshape(tok_rows, 3, 2)
    weights = gate_weight.reshape(tok_rows, 3, 2).astype(jnp.float32)
    chosen = (local_pick[..., None] == jnp.arange(EXP_NODE, dtype=jnp.int32)).astype(jnp.float32)
    slot_meta = (
        jnp.sum(weights[..., None] * chosen, axis=2)
        .reshape(slot_count, EXP_NODE)
        .astype(jnp.bfloat16)
    )
    slot_rows = jnp.concatenate([jnp.repeat(tokens, 3, axis=0), slot_meta], axis=1)
    sent = jnp.dot(place.astype(jnp.bfloat16), slot_rows, preferred_element_type=jnp.float32)
    sent = sent.astype(jnp.bfloat16).reshape(node_count, node_cap, feature_dim + EXP_NODE)
    got = swap(sent, "node").reshape(node_slots, feature_dim + EXP_NODE)
    got_meta = got[:, feature_dim:]
    is_live = got_meta > 0
    live_rank = jnp.cumsum(is_live.astype(jnp.int32), axis=0) - 1
    cap_ids = jnp.arange(slot_count, dtype=jnp.int32)[None, :, None]
    pick_table = is_live.T[:, None, :] & (live_rank.T[:, None, :] == cap_ids)
    pick_table = pick_table.reshape(EXP_NODE * slot_count, node_slots)
    packed = jnp.dot(
        pick_table.astype(jnp.bfloat16), got[:, :feature_dim], preferred_element_type=jnp.float32
    ).astype(jnp.bfloat16)
    quads = slot_count // 4
    outgoing = packed.reshape(EXP_NODE, quads, 4, slices, width).transpose(0, 3, 1, 2, 4)
    arrived = swap(outgoing.reshape(dev_count, quads, 4, width), ("e", "s"))
    rows = arrived.reshape(all_rows, width)

    acts = partial_acts(order, rows, blocks)
    acts = swap(acts, "s")
    acts = jnp.sum(acts.astype(jnp.float32), axis=0)
    hidden = (jax.nn.silu(acts[:hidden_rows]) * acts[hidden_rows:]).astype(jnp.bfloat16)
    hidden = lax.all_gather(hidden, "s", axis=0)
    made = down_rows(order, hidden, blocks)
    returned = swap(made.reshape(dev_count, quads, 4, width), ("e", "s"))
    expert_out = returned.reshape(EXP_NODE, slices, slot_count, width).transpose(0, 2, 1, 3)
    expert_out = expert_out.reshape(EXP_NODE * slot_count, feature_dim)
    combine = pick_table.T.astype(jnp.bfloat16) * jnp.repeat(got_meta, slot_count, axis=1)
    node_out = jnp.dot(combine, expert_out, preferred_element_type=jnp.float32)
    node_out = node_out.astype(jnp.bfloat16).reshape(node_count, node_cap, feature_dim)
    home_rows = swap(node_out, "node").reshape(node_slots, feature_dim)
    return jnp.dot(home.T, home_rows, preferred_element_type=jnp.float32).astype(jnp.bfloat16)


def solution(mesh):
    slices = mesh.shape["dev"] // EXP_NODE
    fine = Mesh(mesh.devices.reshape(mesh.shape["node"], EXP_NODE, slices), ALL)
    spec = P(ALL, None)
    return jax.shard_map(on_device, mesh=fine, in_specs=(spec,) * 7, out_specs=spec, check_vma=False)
```

profile of v0, /device:TPU:16, one launch (start us, length us, event | category | flops | bytes accessed | tf_op | source)
XLA Modules:
  0.0 295.1 jit_solution(15107479518344682043)
XLA Ops:
  0.0 0.8 eq.71
  0.8 0.2 convert_reduce_fusion.1
  1.0 0.8 copy.40
  1.7 0.8 copy.41
  2.5 0.1 select_reduce_fusion
  2.6 0.8 broadcast_in_dim.4
  3.5 0.1 reshape.74
  3.6 0.3 convolution_convert_fusion
  3.9 1.1 reshape.75
  5.0 22.0 %all-to-all-start = ((bf16[32,2,5124]{2,1,0:T(2,128)(2,1)}), bf16[32,2,5124]{2,1,0:T(2,128)(2,1)S(1)}, u32[]{:S(2)}, u32[]{:S(2)}) async-start(bf16[32,2,5124]{2,1,0:T(2,128)(2,1)} %reshape.75), calls=%async_computation | async-start | bytes 1343488 | tf_op jit(solution)/shard_map/all_to_all | solution.py:15
  27.0 0.1 eq.87
  27.1 23.3 %all-to-all-done = bf16[32,2,5124]{2,1,0:T(2,128)(2,1)S(1)} async-done(((bf16[32,2,5124]{2,1,0:T(2,128)(2,1)}), bf16[32,2,5124]{2,1,0:T(2,128)(2,1)S(1)}, u32[]{:S(2)}, u32[]{:S(2)}) %all-to-all-start) | async-done | bytes 655904 | tf_op jit(solution)/shard_map/all_to_all | solution.py:15
  50.4 0.5 reshape.76
  50.9 0.1 reduce_window_sum.11
  51.0 0.1 copy.45
  51.1 0.1 copy.44
  51.3 0.1 compare_and_fusion
  51.3 0.3 convolution_convert_fusion.2
  51.6 0.1 copy.52
  51.7 1.0 copy.47
  52.6 8.8 %all-to-all-start.1 = ((bf16[32,3,4,640]{3,2,1,0:T(4,128)(2,1)}), bf16[32,3,4,640]{3,2,1,0:T(4,128)(2,1)S(1)}, u32[]{:S(2)}, u32[]{:S(2)}) async-start(bf16[32,3,4,640]{3,2,1,0:T(4,128)(2,1)} %bitcast.4), calls=%async_computation.1 | async-start | bytes 983040 | tf_op jit(solution)/shard_map/all_to_all | solution.py:15
  61.4 0.5 iota_xor_fusion.order
  61.9 91.3 %cut_weights.1 = (bf16[288,640]{1,0:T(8,128)(2,1)}, bf16[288,640]{1,0:T(8,128)(2,1)}, bf16[288,640]{1,0:T(8,128)(2,1)}, bf16[288,640]{1,0:T(8,128)(2,1)}, bf16[2...) custom-call(s32[8]{0:T(128)} %iota_xor_fusion.order, ...), custom_call_target="tpu_custom_call" | custom-call | tf_op jit(solution)/shard_map/cut_weights/pallas_call | solution.py:44
  153.3 2.2 collective-permute-start
  155.5 3.5 %collective-permute-start.1 = (bf16[288,640]{1,0:T(8,128)(2,1)}, bf16[288,640]{1,0:T(8,128)(2,1)S(1)}, u32[]{:S(2)}, u32[]{:S(2)}) collective-permute-start(bf16[288,640]{1,0:T(8,128)(2,1)} %get-tuple-element.15), channel_id=1, source_target_pairs={{0,2},{1,3},{2,0},{3,1},{4,6},{5,7},{6,4},{7,5},{8,10},{9,11},{10,... | collective-permute-start | bytes 1105928 | tf_op jit(solution)/shard_map/ppermute | solution.py:126
  159.0 1.9 collective-permute-start.2
  160.9 3.6 %collective-permute-start.3 = (bf16[288,640]{1,0:T(8,128)(2,1)}, bf16[288,640]{1,0:T(8,128)(2,1)S(1)}, u32[]{:S(2)}, u32[]{:S(2)}) collective-permute-start(bf16[288,640]{1,0:T(8,128)(2,1)} %get-tuple-element.17), channel_id=1, source_target_pairs={{0,4},{1,5},{2,6},{3,7},{4,0},{5,1},{6,2},{7,3},{8,12},{9,13},{10,... | collective-permute-start | bytes 1105928 | tf_op jit(solution)/shard_map/ppermute | solution.py:126
  164.6 2.0 collective-permute-start.4
  166.6 0.0 collective-permute-done.refs_1_
  166.6 0.0 copy-start
  166.6 4.4 %collective-permute-start.5 = (bf16[288,640]{1,0:T(8,128)(2,1)}, bf16[288,640]{1,0:T(8,128)(2,1)S(1)}, u32[]{:S(2)}, u32[]{:S(2)}) collective-permute-start(bf16[288,640]{1,0:T(8,128)(2,1)} %get-tuple-element.19), channel_id=1, source_target_pairs={{0,6},{1,7},{2,4},{3,5},{4,2},{5,3},{6,0},{7,1},{8,14},{9,15},{10,... | collective-permute-start | bytes 1105928 | tf_op jit(solution)/shard_map/ppermute | solution.py:126
  171.1 0.0 collective-permute-done.1.refs_2_
  171.1 1.9 collective-permute-start.6
  173.0 0.0 all-to-all-done.1
  173.0 0.9 reshape.80.rows
  174.0 1.6 collective-permute-done.2.refs_3_
  175.6 0.0 collective-permute-done.3.refs_4_
  175.6 6.1 %collective-permute-done.4.refs_5_ = bf16[288,640]{1,0:T(8,128)(2,1)S(1)} collective-permute-done((bf16[288,640]{1,0:T(8,128)(2,1)}, bf16[288,640]{1,0:T(8,128)(2,1)S(1)}, u32[]{:S(2)}, u32[]{:S(2)}) %collective-permute-start.4) | collective-permute-done | bytes 368672 | tf_op jit(solution)/shard_map/ppermute | solution.py:126
  181.8 9.7 %collective-permute-done.5.refs_6_ = bf16[288,640]{1,0:T(8,128)(2,1)S(1)} collective-permute-done((bf16[288,640]{1,0:T(8,128)(2,1)}, bf16[288,640]{1,0:T(8,128)(2,1)S(1)}, u32[]{:S(2)}, u32[]{:S(2)}) %collective-permute-start.5) | collective-permute-done | bytes 368672 | tf_op jit(solution)/shard_map/ppermute | solution.py:126
  191.5 6.9 %collective-permute-done.6.refs_7_ = bf16[288,640]{1,0:T(8,128)(2,1)} collective-permute-done((bf16[288,640]{1,0:T(8,128)(2,1)}, bf16[288,640]{1,0:T(8,128)(2,1)}, u32[]{:S(2)}, u32[]{:S(2)}) %collective-permute-start.6) | collective-permute-done | bytes 368672 | tf_op jit(solution)/shard_map/ppermute | solution.py:126
  198.3 0.0 copy-done
  198.3 0.0 copy-done.2
  198.4 4.1 %partial_acts.1 = bf16[8,192,384]{2,1,0:T(8,128)(2,1)} custom-call(s32[8]{0:T(128)} %iota_xor_fusion.order, bf16[384,640]{1,0:T(8,128)(2,1)} %reshape.80.rows, bf16[288,640]{1,0:T(8,128)(2,1)} %get-tuple-element.13.refs_0_, bf16[288,640]{1,0:T(8,128)(2,1)} %copy-done, bf16[288,640]{1,0:T(8,128)(2,1)} %copy-done.1, bf16[288,640]{1,0:T(8,128)(2,1)} %copy-done.2, ...), custom_call_target="tpu_custom_call" | custom-call | tf_op jit(solution)/shard_map/partial_acts/pallas_call | solution.py:69
  202.5 20.0 %all_to_all.25 = bf16[8,192,384]{2,1,0:T(8,128)(2,1)S(1)} all-to-all(bf16[8,192,384]{2,1,0:T(8,128)(2,1)} %partial_acts.1), channel_id=1, replica_groups=mesh['node'=32,'e'=4,'s'=8] {'s'}, dimensions={0} | all-to-all | bytes 2359296 | tf_op jit(solution)/shard_map/all_to_all | solution.py:15
  222.5 0.2 convert_reduce_fusion
  222.7 0.1 fusion.4
  222.7 13.7 %all-gather = bf16[768,384]{1,0:T(8,128)(2,1)} all-gather(bf16[96,384]{1,0:T(8,128)(2,1)S(1)} %fusion.4), channel_id=2, replica_groups=mesh['node'=32,'e'=4,'s'=8] {'s'}, dimensions={0}, use_global_device_ids=true | all-gather | bytes 663552 | tf_op jit(solution)/shard_map/all_gather | solution.py:167
  236.4 2.9 down_rows.1
  239.3 1.9 reshape.81
  241.2 7.4 %all-to-all-start.3 = ((bf16[32,3,4,640]{3,2,1,0:T(4,128)(2,1)}), bf16[32,3,4,640]{3,2,1,0:T(4,128)(2,1)S(1)}, u32[]{:S(2)}, u32[]{:S(2)}) async-start(bf16[32,3,4,640]{3,2,1,0:T(4,128)(2,1)} %reshape.81), calls=%async_computation.3 | async-start | bytes 983040 | tf_op jit(solution)/shard_map/all_to_all | solution.py:15
  248.6 0.1 copy.46
  248.7 17.2 %all-to-all-done.3 = bf16[32,3,4,640]{3,2,1,0:T(4,128)(2,1)S(1)} async-done(((bf16[32,3,4,640]{3,2,1,0:T(4,128)(2,1)}), bf16[32,3,4,640]{3,2,1,0:T(4,128)(2,1)S(1)}, u32[]{:S(2)}, u32[]{:S(2)}) %all-to-all-start.3) | async-done | bytes 491552 | tf_op jit(solution)/shard_map/all_to_all | solution.py:15
  265.9 0.1 copy.48
  266.0 0.1 copy.53
  266.1 0.4 convolution_convert_fusion.1
  266.4 0.0 copy-start.6
  266.5 1.1 reshape.84
  267.5 4.6 %all-to-all-start.4 = ((bf16[32,2,5120]{2,1,0:T(2,128)(2,1)}), bf16[32,2,5120]{2,1,0:T(2,128)(2,1)S(1)}, u32[]{:S(2)}, u32[]{:S(2)}) async-start(bf16[32,2,5120]{2,1,0:T(2,128)(2,1)} %reshape.84), calls=%async_computation.4 | async-start | bytes 1310720 | tf_op jit(solution)/shard_map/all_to_all | solution.py:15
  272.1 0.1 reduce_sum.42
  272.2 0.1 copy.39
  272.3 0.1 fusion.9
  272.4 21.7 %all-to-all-done.4 = bf16[32,2,5120]{2,1,0:T(2,128)(2,1)S(1)} async-done(((bf16[32,2,5120]{2,1,0:T(2,128)(2,1)}), bf16[32,2,5120]{2,1,0:T(2,128)(2,1)S(1)}, u32[]{:S(2)}, u32[]{:S(2)}) %all-to-all-start.4) | async-done | bytes 655392 | tf_op jit(solution)/shard_map/all_to_all | solution.py:15
  294.0 0.2 reshape.85
  294.3 0.8 convolution_convert_fusion.3
  (27 shorter events, 0.2 us)
Async XLA Ops:
  5.0 45.4 %all-to-all-start = ((bf16[32,2,5124]{2,1,0:T(2,128)(2,1)}), bf16[32,2,5124]{2,1,0:T(2,128)(2,1)S(1)}, u32[]{:S(2)}, u32[]{:S(2)}) async-start(bf16[32,2,5124]{2,1,0:T(2,128)(2,1)} %reshape.75), calls=%async_computation | async-start | bytes 1343488 | tf_op jit(solution)/shard_map/all_to_all | solution.py:15
  52.6 120.4 %all-to-all-start.1 = ((bf16[32,3,4,640]{3,2,1,0:T(4,128)(2,1)}), bf16[32,3,4,640]{3,2,1,0:T(4,128)(2,1)S(1)}, u32[]{:S(2)}, u32[]{:S(2)}) async-start(bf16[32,3,4,640]{3,2,1,0:T(4,128)(2,1)} %bitcast.4), calls=%async_computation.1 | async-start | bytes 983040 | tf_op jit(solution)/shard_map/all_to_all | solution.py:15
  153.3 13.3 %collective-permute-start = (bf16[288,640]{1,0:T(8,128)(2,1)}, bf16[288,640]{1,0:T(8,128)(2,1)S(1)}, u32[]{:S(2)}, u32[]{:S(2)}) collective-permute-start(bf16[288,640]{1,0:T(8,128)(2,1)} %get-tuple-element.14), channel_id=1, source_target_pairs={{0,1},{1,0},{2,3},{3,2},{4,5},{5,4},{6,7},{7,6},{8,9},{9,8},{10,11... | collective-permute-start | bytes 1105928 | tf_op jit(solution)/shard_map/ppermute | solution.py:126
  155.5 15.6 %collective-permute-start.1 = (bf16[288,640]{1,0:T(8,128)(2,1)}, bf16[288,640]{1,0:T(8,128)(2,1)S(1)}, u32[]{:S(2)}, u32[]{:S(2)}) collective-permute-start(bf16[288,640]{1,0:T(8,128)(2,1)} %get-tuple-element.15), channel_id=1, source_target_pairs={{0,2},{1,3},{2,0},{3,1},{4,6},{5,7},{6,4},{7,5},{8,10},{9,11},{10,... | collective-permute-start | bytes 1105928 | tf_op jit(solution)/shard_map/ppermute | solution.py:126
  159.0 16.6 %collective-permute-start.2 = (bf16[288,640]{1,0:T(8,128)(2,1)}, bf16[288,640]{1,0:T(8,128)(2,1)S(1)}, u32[]{:S(2)}, u32[]{:S(2)}) collective-permute-start(bf16[288,640]{1,0:T(8,128)(2,1)} %get-tuple-element.16), channel_id=1, source_target_pairs={{0,3},{1,2},{2,1},{3,0},{4,7},{5,6},{6,5},{7,4},{8,11},{9,10},{10,... | collective-permute-start | bytes 1105928 | tf_op jit(solution)/shard_map/ppermute | solution.py:126
  160.9 14.7 %collective-permute-start.3 = (bf16[288,640]{1,0:T(8,128)(2,1)}, bf16[288,640]{1,0:T(8,128)(2,1)S(1)}, u32[]{:S(2)}, u32[]{:S(2)}) collective-permute-start(bf16[288,640]{1,0:T(8,128)(2,1)} %get-tuple-element.17), channel_id=1, source_target_pairs={{0,4},{1,5},{2,6},{3,7},{4,0},{5,1},{6,2},{7,3},{8,12},{9,13},{10,... | collective-permute-start | bytes 1105928 | tf_op jit(solution)/shard_map/ppermute | solution.py:126
  164.6 17.2 %collective-permute-start.4 = (bf16[288,640]{1,0:T(8,128)(2,1)}, bf16[288,640]{1,0:T(8,128)(2,1)S(1)}, u32[]{:S(2)}, u32[]{:S(2)}) collective-permute-start(bf16[288,640]{1,0:T(8,128)(2,1)} %get-tuple-element.18), channel_id=1, source_target_pairs={{0,5},{1,4},{2,7},{3,6},{4,1},{5,0},{6,3},{7,2},{8,13},{9,12},{10,... | collective-permute-start | bytes 1105928 | tf_op jit(solution)/shard_map/ppermute | solution.py:126
  166.6 31.7 %copy-start = (bf16[288,640]{1,0:T(8,128)(2,1)}, bf16[288,640]{1,0:T(8,128)(2,1)S(1)}, u32[]{:S(2)}) copy-start(bf16[288,640]{1,0:T(8,128)(2,1)S(1)} %collective-permute-done.refs_1_) | copy-start | bytes 1105924
  166.6 24.8 %collective-permute-start.5 = (bf16[288,640]{1,0:T(8,128)(2,1)}, bf16[288,640]{1,0:T(8,128)(2,1)S(1)}, u32[]{:S(2)}, u32[]{:S(2)}) collective-permute-start(bf16[288,640]{1,0:T(8,128)(2,1)} %get-tuple-element.19), channel_id=1, source_target_pairs={{0,6},{1,7},{2,4},{3,5},{4,2},{5,3},{6,0},{7,1},{8,14},{9,15},{10,... | collective-permute-start | bytes 1105928 | tf_op jit(solution)/shard_map/ppermute | solution.py:126
  171.1 27.2 %copy-start.1 = (bf16[288,640]{1,0:T(8,128)(2,1)}, bf16[288,640]{1,0:T(8,128)(2,1)S(1)}, u32[]{:S(2)}) copy-start(bf16[288,640]{1,0:T(8,128)(2,1)S(1)} %collective-permute-done.1.refs_2_) | copy-start | bytes 1105924
  171.1 27.2 %collective-permute-start.6 = (bf16[288,640]{1,0:T(8,128)(2,1)}, bf16[288,640]{1,0:T(8,128)(2,1)}, u32[]{:S(2)}, u32[]{:S(2)}) collective-permute-start(bf16[288,640]{1,0:T(8,128)(2,1)} %get-tuple-element.20), channel_id=1, source_target_pairs={{0,7},{1,6},{2,5},{3,4},{4,3},{5,2},{6,1},{7,0},{8,15},{9,14},{10,... | collective-permute-start | bytes 1105928 | tf_op jit(solution)/shard_map/ppermute | solution.py:126
  175.6 22.7 %copy-start.2 = (bf16[288,640]{1,0:T(8,128)(2,1)}, bf16[288,640]{1,0:T(8,128)(2,1)S(1)}, u32[]{:S(2)}) copy-start(bf16[288,640]{1,0:T(8,128)(2,1)S(1)} %collective-permute-done.2.refs_3_) | copy-start | bytes 1105924
  175.6 22.7 %copy-start.3 = (bf16[288,640]{1,0:T(8,128)(2,1)}, bf16[288,640]{1,0:T(8,128)(2,1)S(1)}, u32[]{:S(2)}) copy-start(bf16[288,640]{1,0:T(8,128)(2,1)S(1)} %collective-permute-done.3.refs_4_) | copy-start | bytes 1105924
  181.8 16.6 %copy-start.4 = (bf16[288,640]{1,0:T(8,128)(2,1)}, bf16[288,640]{1,0:T(8,128)(2,1)S(1)}, u32[]{:S(2)}) copy-start(bf16[288,640]{1,0:T(8,128)(2,1)S(1)} %collective-permute-done.4.refs_5_) | copy-start | bytes 1105924
  191.5 6.9 %copy-start.5 = (bf16[288,640]{1,0:T(8,128)(2,1)}, bf16[288,640]{1,0:T(8,128)(2,1)S(1)}, u32[]{:S(2)}) copy-start(bf16[288,640]{1,0:T(8,128)(2,1)S(1)} %collective-permute-done.5.refs_6_) | copy-start | bytes 1105924
  241.2 24.7 %all-to-all-start.3 = ((bf16[32,3,4,640]{3,2,1,0:T(4,128)(2,1)}), bf16[32,3,4,640]{3,2,1,0:T(4,128)(2,1)S(1)}, u32[]{:S(2)}, u32[]{:S(2)}) async-start(bf16[32,3,4,640]{3,2,1,0:T(4,128)(2,1)} %reshape.81), calls=%async_computation.3 | async-start | bytes 983040 | tf_op jit(solution)/shard_map/all_to_all | solution.py:15
  266.4 5.8 %copy-start.6 = (s32[4,3]{1,0:T(4,128)S(1)}, s32[4,3]{1,0:T(4,128)}, u32[]{:S(2)}) copy-start(s32[4,3]{1,0:T(4,128)} %param.8) | copy-start | bytes 148
  267.5 26.5 %all-to-all-start.4 = ((bf16[32,2,5120]{2,1,0:T(2,128)(2,1)}), bf16[32,2,5120]{2,1,0:T(2,128)(2,1)S(1)}, u32[]{:S(2)}, u32[]{:S(2)}) async-start(bf16[32,2,5120]{2,1,0:T(2,128)(2,1)} %reshape.84), calls=%async_computation.4 | async-start | bytes 1310720 | tf_op jit(solution)/shard_map/all_to_all | solution.py:15
where the time goes:
time: 296 us; the launch traced here: 295 us
  Pallas kernels  98.3 us (33%)
  waiting for transfers between devices  86.5 us (29%)
  starting transfers between devices  62.4 us (21%)
  blocking collectives  33.7 us (11%)
  local copies, waits for them, and re-layouts  10.9 us (4%)
    pallas_call x1, Pallas kernels, cut_weights(): pl.pallas_call(cut_kernel, in_specs=[pl.BlockSpec(memory_space=pltpu.SMEM...  91.3 us
    all_to_all x4, waiting for transfers between devices, swap(): return lax.all_to_all(a, axis, split_axis=0, concat_axis=0, tiled=True)  62.1 us
    all_to_all x4, starting transfers between devices, swap(): return lax.all_to_all(a, axis, split_axis=0, concat_axis=0, tiled=True)  42.7 us
    ppermute x7, waiting for transfers between devices, on_device(): lax.ppermute(cut[k], 's', [(a, a ^ k) for a in range(slices)])  24.3 us
    all_to_all x1, blocking collectives, swap(): return lax.all_to_all(a, axis, split_axis=0, concat_axis=0, tiled=True)  20 us
    ppermute x7, starting transfers between devices, on_device(): lax.ppermute(cut[k], 's', [(a, a ^ k) for a in range(slices)])  19.7 us
    all_gather x1, blocking collectives, on_device(): hidden = lax.all_gather(hidden, 's', axis=0)  13.7 us
  transfers between devices with their start and end apart: 11, of which 7 were waited for; matrix products, arithmetic and copies ran while one was open for 1% of the time, Pallas kernels for 31%

commit v1 on v0

--- a/solution.py
+++ b/solution.py
@@ -16,25 +16,31 @@
 
 
 def cut_kernel(order, gate, up, down, *refs):
-    outs, sem = refs[:-1], refs[-1]
+    outs, (hold, read_sem, write_sem) = refs[:-3], refs[-3:]
     parts = len(outs)
     rows = gate.shape[0]
     width = gate.shape[1] // parts
-    copies = []
+    reads = []
     for k in range(parts):
         column = pl.multiple_of(order[k] * width, width)
         for i, source in enumerate((gate, up, down)):
-            copies.append(
+            reads.append(
                 pltpu.make_async_copy(
                     source.at[:, pl.ds(column, width)],
-                    outs[k].at[pl.ds(i * rows, rows), :],
-                    sem.at[3 * k + i],
+                    hold.at[k, pl.ds(i * rows, rows), :],
+                    read_sem.at[3 * k + i],
                 )
             )
-    for copy in copies:
-        copy.start()
-    for copy in copies:
-        copy.wait()
+    for read in reads:
+        read.start()
+    writes = []
+    for k in range(parts):
+        for read in reads[3 * k : 3 * k + 3]:
+            read.wait()
+        writes.append(pltpu.make_async_copy(hold.at[k], outs[k], write_sem.at[k]))
+        writes[-1].start()
+    for write in writes:
+        write.wait()
 
 
 def cut_weights(order, w_gate, w_up, w_down, parts):
@@ -46,7 +52,11 @@
         in_specs=[pl.BlockSpec(memory_space=pltpu.SMEM)] + [anywhere] * 3,
         out_specs=[anywhere] * parts,
         out_shape=[jax.ShapeDtypeStruct((3 * rows, width), w_gate.dtype)] * parts,
-        scratch_shapes=[pltpu.SemaphoreType.DMA((3 * parts,))],
+        scratch_shapes=[
+            pltpu.VMEM((parts, 3 * rows, width), w_gate.dtype),
+            pltpu.SemaphoreType.DMA((3 * parts,)),
+            pltpu.SemaphoreType.DMA((parts,)),
+        ],
         name="cut_weights",
     )(order, w_gate, w_up, w_down)
 

time: 296 us -> 208 us (0.70)
  Pallas kernels: 98.3 us -> 10.6 us
    pallas_call x1, Pallas kernels: 91.3 us -> 3.64 us  [cut_weights(): pl.pallas_call(cut_kernel, in_specs=[pl.BlockSpec(memory_space=pltpu.SMEM...]
  transfers between devices with their start and end apart: 11 -> 11, of which waited for: 7 -> 7; matrix products, arithmetic and copies ran while one was open for 1% -> 1% of each run, Pallas kernels for 31% -> 2%
where the time goes in v1:
time: 208 us; the launch traced here: 207 us
  waiting for transfers between devices  86.1 us (41%)
  starting transfers between devices  62.7 us (30%)
  blocking collectives  33.7 us (16%)
  local copies, waits for them, and re-layouts  10.9 us (5%)
  Pallas kernels  10.6 us (5%)
    all_to_all x4, waiting for transfers between devices, swap(): return lax.all_to_all(a, axis, split_axis=0, concat_axis=0, tiled=True)  62.1 us
    all_to_all x4, starting transfers between devices, swap(): return lax.all_to_all(a, axis, split_axis=0, concat_axis=0, tiled=True)  42.7 us
    ppermute x7, waiting for transfers between devices, on_device(): lax.ppermute(cut[k], 's', [(a, a ^ k) for a in range(slices)])  24 us
    ppermute x7, starting transfers between devices, on_device(): lax.ppermute(cut[k], 's', [(a, a ^ k) for a in range(slices)])  20 us
    all_to_all x1, blocking collectives, swap(): return lax.all_to_all(a, axis, split_axis=0, concat_axis=0, tiled=True)  20 us
    all_gather x1, blocking collectives, on_device(): hidden = lax.all_gather(hidden, 's', axis=0)  13.7 us
  transfers between devices with their start and end apart: 11, of which 7 were waited for; matrix products, arithmetic and copies ran while one was open for 1% of the time, Pallas kernels for 2%

profile of v1, /device:TPU:16, one launch (start us, length us, event | category | flops | bytes accessed | tf_op | source)
XLA Modules:
  0.0 207.4 jit_solution(10162132854175471480)
XLA Ops:
  0.0 0.8 eq.71
  0.8 0.2 convert_reduce_fusion.1
  1.0 0.8 copy.40
  1.7 0.8 copy.41
  2.5 0.1 select_reduce_fusion
  2.6 0.8 broadcast_in_dim.4
  3.5 0.1 reshape.74
  3.6 0.3 convolution_convert_fusion
  3.9 1.1 reshape.75
  5.0 22.0 %all-to-all-start = ((bf16[32,2,5124]{2,1,0:T(2,128)(2,1)}), bf16[32,2,5124]{2,1,0:T(2,128)(2,1)S(1)}, u32[]{:S(2)}, u32[]{:S(2)}) async-start(bf16[32,2,5124]{2,1,0:T(2,128)(2,1)} %reshape.75), calls=%async_computation | async-start | bytes 1343488 | tf_op jit(solution)/shard_map/all_to_all | solution.py:15
  27.0 0.1 eq.87
  27.1 23.3 %all-to-all-done = bf16[32,2,5124]{2,1,0:T(2,128)(2,1)S(1)} async-done(((bf16[32,2,5124]{2,1,0:T(2,128)(2,1)}), bf16[32,2,5124]{2,1,0:T(2,128)(2,1)S(1)}, u32[]{:S(2)}, u32[]{:S(2)}) %all-to-all-start) | async-done | bytes 655904 | tf_op jit(solution)/shard_map/all_to_all | solution.py:15
  50.4 0.5 reshape.76
  50.9 0.1 reduce_window_sum.11
  51.0 0.1 copy.45
  51.1 0.1 copy.44
  51.3 0.1 compare_and_fusion
  51.3 0.3 convolution_convert_fusion.2
  51.6 0.1 copy.52
  51.7 1.0 copy.47
  52.6 8.8 %all-to-all-start.1 = ((bf16[32,3,4,640]{3,2,1,0:T(4,128)(2,1)}), bf16[32,3,4,640]{3,2,1,0:T(4,128)(2,1)S(1)}, u32[]{:S(2)}, u32[]{:S(2)}) async-start(bf16[32,3,4,640]{3,2,1,0:T(4,128)(2,1)} %bitcast.4), calls=%async_computation.1 | async-start | bytes 983040 | tf_op jit(solution)/shard_map/all_to_all | solution.py:15
  61.4 0.5 iota_xor_fusion.order
  61.9 3.6 %cut_weights.1 = (bf16[288,640]{1,0:T(8,128)(2,1)}, bf16[288,640]{1,0:T(8,128)(2,1)}, bf16[288,640]{1,0:T(8,128)(2,1)}, bf16[288,640]{1,0:T(8,128)(2,1)}, bf16[2...) custom-call(s32[8]{0:T(128)} %iota_xor_fusion.order, ...), custom_call_target="tpu_custom_call" | custom-call | tf_op jit(solution)/shard_map/cut_weights/pallas_call | solution.py:50
  65.6 2.2 %collective-permute-start = (bf16[288,640]{1,0:T(8,128)(2,1)}, bf16[288,640]{1,0:T(8,128)(2,1)S(1)}, u32[]{:S(2)}, u32[]{:S(2)}) collective-permute-start(bf16[288,640]{1,0:T(8,128)(2,1)} %get-tuple-element.14), channel_id=1, source_target_pairs={{0,1},{1,0},{2,3},{3,2},{4,5},{5,4},{6,7},{7,6},{8,9},{9,8},{10,11... | collective-permute-start | bytes 1105928 | tf_op jit(solution)/shard_map/ppermute | solution.py:136
  67.8 3.5 %collective-permute-start.1 = (bf16[288,640]{1,0:T(8,128)(2,1)}, bf16[288,640]{1,0:T(8,128)(2,1)S(1)}, u32[]{:S(2)}, u32[]{:S(2)}) collective-permute-start(bf16[288,640]{1,0:T(8,128)(2,1)} %get-tuple-element.15), channel_id=1, source_target_pairs={{0,2},{1,3},{2,0},{3,1},{4,6},{5,7},{6,4},{7,5},{8,10},{9,11},{10,... | collective-permute-start | bytes 1105928 | tf_op jit(solution)/shard_map/ppermute | solution.py:136
  71.3 1.9 collective-permute-start.2
  73.3 3.6 %collective-permute-start.3 = (bf16[288,640]{1,0:T(8,128)(2,1)}, bf16[288,640]{1,0:T(8,128)(2,1)S(1)}, u32[]{:S(2)}, u32[]{:S(2)}) collective-permute-start(bf16[288,640]{1,0:T(8,128)(2,1)} %get-tuple-element.17), channel_id=1, source_target_pairs={{0,4},{1,5},{2,6},{3,7},{4,0},{5,1},{6,2},{7,3},{8,12},{9,13},{10,... | collective-permute-start | bytes 1105928 | tf_op jit(solution)/shard_map/ppermute | solution.py:136
  76.9 2.0 collective-permute-start.4
  78.9 0.0 collective-permute-done.refs_1_
  78.9 0.0 copy-start
  79.0 4.4 %collective-permute-start.5 = (bf16[288,640]{1,0:T(8,128)(2,1)}, bf16[288,640]{1,0:T(8,128)(2,1)S(1)}, u32[]{:S(2)}, u32[]{:S(2)}) collective-permute-start(bf16[288,640]{1,0:T(8,128)(2,1)} %get-tuple-element.19), channel_id=1, source_target_pairs={{0,6},{1,7},{2,4},{3,5},{4,2},{5,3},{6,0},{7,1},{8,14},{9,15},{10,... | collective-permute-start | bytes 1105928 | tf_op jit(solution)/shard_map/ppermute | solution.py:136
  83.4 0.0 collective-permute-done.1.refs_2_
  83.4 2.3 %collective-permute-start.6 = (bf16[288,640]{1,0:T(8,128)(2,1)}, bf16[288,640]{1,0:T(8,128)(2,1)}, u32[]{:S(2)}, u32[]{:S(2)}) collective-permute-start(bf16[288,640]{1,0:T(8,128)(2,1)} %get-tuple-element.20), channel_id=1, source_target_pairs={{0,7},{1,6},{2,5},{3,4},{4,3},{5,2},{6,1},{7,0},{8,15},{9,14},{10,... | collective-permute-start | bytes 1105928 | tf_op jit(solution)/shard_map/ppermute | solution.py:136
  85.7 0.0 all-to-all-done.1
  85.7 0.9 reshape.80.rows
  86.6 3.7 %collective-permute-done.2.refs_3_ = bf16[288,640]{1,0:T(8,128)(2,1)S(1)} collective-permute-done((bf16[288,640]{1,0:T(8,128)(2,1)}, bf16[288,640]{1,0:T(8,128)(2,1)S(1)}, u32[]{:S(2)}, u32[]{:S(2)}) %collective-permute-start.2) | collective-permute-done | bytes 368672 | tf_op jit(solution)/shard_map/ppermute | solution.py:136
  90.3 0.0 collective-permute-done.3.refs_4_
  90.3 3.8 %collective-permute-done.4.refs_5_ = bf16[288,640]{1,0:T(8,128)(2,1)S(1)} collective-permute-done((bf16[288,640]{1,0:T(8,128)(2,1)}, bf16[288,640]{1,0:T(8,128)(2,1)S(1)}, u32[]{:S(2)}, u32[]{:S(2)}) %collective-permute-start.4) | collective-permute-done | bytes 368672 | tf_op jit(solution)/shard_map/ppermute | solution.py:136
  94.1 9.7 %collective-permute-done.5.refs_6_ = bf16[288,640]{1,0:T(8,128)(2,1)S(1)} collective-permute-done((bf16[288,640]{1,0:T(8,128)(2,1)}, bf16[288,640]{1,0:T(8,128)(2,1)S(1)}, u32[]{:S(2)}, u32[]{:S(2)}) %collective-permute-start.5) | collective-permute-done | bytes 368672 | tf_op jit(solution)/shard_map/ppermute | solution.py:136
  103.8 6.9 %collective-permute-done.6.refs_7_ = bf16[288,640]{1,0:T(8,128)(2,1)} collective-permute-done((bf16[288,640]{1,0:T(8,128)(2,1)}, bf16[288,640]{1,0:T(8,128)(2,1)}, u32[]{:S(2)}, u32[]{:S(2)}) %collective-permute-start.6) | collective-permute-done | bytes 368672 | tf_op jit(solution)/shard_map/ppermute | solution.py:136
  110.6 0.0 copy-done.1
  110.7 4.1 %partial_acts.1 = bf16[8,192,384]{2,1,0:T(8,128)(2,1)} custom-call(s32[8]{0:T(128)} %iota_xor_fusion.order, bf16[384,640]{1,0:T(8,128)(2,1)} %reshape.80.rows, bf16[288,640]{1,0:T(8,128)(2,1)} %get-tuple-element.13.refs_0_, bf16[288,640]{1,0:T(8,128)(2,1)} %copy-done, bf16[288,640]{1,0:T(8,128)(2,1)} %copy-done.1, bf16[288,640]{1,0:T(8,128)(2,1)} %copy-done.2, ...), custom_call_target="tpu_custom_call" | custom-call | tf_op jit(solution)/shard_map/partial_acts/pallas_call | solution.py:79
  114.8 20.0 %all_to_all.25 = bf16[8,192,384]{2,1,0:T(8,128)(2,1)S(1)} all-to-all(bf16[8,192,384]{2,1,0:T(8,128)(2,1)} %partial_acts.1), channel_id=1, replica_groups=mesh['node'=32,'e'=4,'s'=8] {'s'}, dimensions={0} | all-to-all | bytes 2359296 | tf_op jit(solution)/shard_map/all_to_all | solution.py:15
  134.8 0.2 convert_reduce_fusion
  135.0 0.1 fusion.4
  135.0 13.7 %all-gather = bf16[768,384]{1,0:T(8,128)(2,1)} all-gather(bf16[96,384]{1,0:T(8,128)(2,1)S(1)} %fusion.4), channel_id=2, replica_groups=mesh['node'=32,'e'=4,'s'=8] {'s'}, dimensions={0}, use_global_device_ids=true | all-gather | bytes 663552 | tf_op jit(solution)/shard_map/all_gather | solution.py:177
  148.7 2.9 %down_rows.1 = bf16[384,640]{1,0:T(8,128)(2,1)} custom-call(s32[8]{0:T(128)} %iota_xor_fusion.order, bf16[8,96,384]{2,1,0:T(8,128)(2,1)} %bitcast.30, bf16[288,640]{1,0:T(8,128)(2,1)} %get-tuple-element.13.refs_0_, bf16[288,640]{1,0:T(8,128)(2,1)} %copy-done, bf16[288,640]{1,0:T(8,128)(2,1)} %copy-done.1, bf16[288,640]{1,0:T(8,128)(2,1)} %copy-done.2, ...), custom_call_target="tpu_custom_call" | custom-call | tf_op jit(solution)/shard_map/down_rows/pallas_call | solution.py:105
  151.6 1.9 reshape.81
  153.5 7.4 %all-to-all-start.3 = ((bf16[32,3,4,640]{3,2,1,0:T(4,128)(2,1)}), bf16[32,3,4,640]{3,2,1,0:T(4,128)(2,1)S(1)}, u32[]{:S(2)}, u32[]{:S(2)}) async-start(bf16[32,3,4,640]{3,2,1,0:T(4,128)(2,1)} %reshape.81), calls=%async_computation.3 | async-start | bytes 983040 | tf_op jit(solution)/shard_map/all_to_all | solution.py:15
  160.9 0.1 copy.46
  161.0 17.2 %all-to-all-done.3 = bf16[32,3,4,640]{3,2,1,0:T(4,128)(2,1)S(1)} async-done(((bf16[32,3,4,640]{3,2,1,0:T(4,128)(2,1)}), bf16[32,3,4,640]{3,2,1,0:T(4,128)(2,1)S(1)}, u32[]{:S(2)}, u32[]{:S(2)}) %all-to-all-start.3) | async-done | bytes 491552 | tf_op jit(solution)/shard_map/all_to_all | solution.py:15
  178.2 0.1 copy.48
  178.3 0.1 copy.53
  178.4 0.4 convolution_convert_fusion.1
  178.8 0.0 copy-start.6
  178.8 1.1 reshape.84
  179.9 4.6 %all-to-all-start.4 = ((bf16[32,2,5120]{2,1,0:T(2,128)(2,1)}), bf16[32,2,5120]{2,1,0:T(2,128)(2,1)S(1)}, u32[]{:S(2)}, u32[]{:S(2)}) async-start(bf16[32,2,5120]{2,1,0:T(2,128)(2,1)} %reshape.84), calls=%async_computation.4 | async-start | bytes 1310720 | tf_op jit(solution)/shard_map/all_to_all | solution.py:15
  184.4 0.1 reduce_sum.42
  184.5 0.0 copy-done.6
  184.5 0.1 copy.39
  184.6 0.1 fusion.9
  184.7 21.7 %all-to-all-done.4 = bf16[32,2,5120]{2,1,0:T(2,128)(2,1)S(1)} async-done(((bf16[32,2,5120]{2,1,0:T(2,128)(2,1)}), bf16[32,2,5120]{2,1,0:T(2,128)(2,1)S(1)}, u32[]{:S(2)}, u32[]{:S(2)}) %all-to-all-start.4) | async-done | bytes 655392 | tf_op jit(solution)/shard_map/all_to_all | solution.py:15
  206.3 0.2 reshape.85
  206.6 0.8 convolution_convert_fusion.3
  (27 shorter events, 0.2 us)
Async XLA Ops:
  5.0 45.4 %all-to-all-start = ((bf16[32,2,5124]{2,1,0:T(2,128)(2,1)}), bf16[32,2,5124]{2,1,0:T(2,128)(2,1)S(1)}, u32[]{:S(2)}, u32[]{:S(2)}) async-start(bf16[32,2,5124]{2,1,0:T(2,128)(2,1)} %reshape.75), calls=%async_computation | async-start | bytes 1343488 | tf_op jit(solution)/shard_map/all_to_all | solution.py:15
  52.6 33.1 %all-to-all-start.1 = ((bf16[32,3,4,640]{3,2,1,0:T(4,128)(2,1)}), bf16[32,3,4,640]{3,2,1,0:T(4,128)(2,1)S(1)}, u32[]{:S(2)}, u32[]{:S(2)}) async-start(bf16[32,3,4,640]{3,2,1,0:T(4,128)(2,1)} %bitcast.4), calls=%async_computation.1 | async-start | bytes 983040 | tf_op jit(solution)/shard_map/all_to_all | solution.py:15
  65.6 13.3 %collective-permute-start = (bf16[288,640]{1,0:T(8,128)(2,1)}, bf16[288,640]{1,0:T(8,128)(2,1)S(1)}, u32[]{:S(2)}, u32[]{:S(2)}) collective-permute-start(bf16[288,640]{1,0:T(8,128)(2,1)} %get-tuple-element.14), channel_id=1, source_target_pairs={{0,1},{1,0},{2,3},{3,2},{4,5},{5,4},{6,7},{7,6},{8,9},{9,8},{10,11... | collective-permute-start | bytes 1105928 | tf_op jit(solution)/shard_map/ppermute | solution.py:136
  67.8 15.6 %collective-permute-start.1 = (bf16[288,640]{1,0:T(8,128)(2,1)}, bf16[288,640]{1,0:T(8,128)(2,1)S(1)}, u32[]{:S(2)}, u32[]{:S(2)}) collective-permute-start(bf16[288,640]{1,0:T(8,128)(2,1)} %get-tuple-element.15), channel_id=1, source_target_pairs={{0,2},{1,3},{2,0},{3,1},{4,6},{5,7},{6,4},{7,5},{8,10},{9,11},{10,... | collective-permute-start | bytes 1105928 | tf_op jit(solution)/shard_map/ppermute | solution.py:136
  71.3 19.0 %collective-permute-start.2 = (bf16[288,640]{1,0:T(8,128)(2,1)}, bf16[288,640]{1,0:T(8,128)(2,1)S(1)}, u32[]{:S(2)}, u32[]{:S(2)}) collective-permute-start(bf16[288,640]{1,0:T(8,128)(2,1)} %get-tuple-element.16), channel_id=1, source_target_pairs={{0,3},{1,2},{2,1},{3,0},{4,7},{5,6},{6,5},{7,4},{8,11},{9,10},{10,... | collective-permute-start | bytes 1105928 | tf_op jit(solution)/shard_map/ppermute | solution.py:136
  73.3 17.1 %collective-permute-start.3 = (bf16[288,640]{1,0:T(8,128)(2,1)}, bf16[288,640]{1,0:T(8,128)(2,1)S(1)}, u32[]{:S(2)}, u32[]{:S(2)}) collective-permute-start(bf16[288,640]{1,0:T(8,128)(2,1)} %get-tuple-element.17), channel_id=1, source_target_pairs={{0,4},{1,5},{2,6},{3,7},{4,0},{5,1},{6,2},{7,3},{8,12},{9,13},{10,... | collective-permute-start | bytes 1105928 | tf_op jit(solution)/shard_map/ppermute | solution.py:136
  76.9 17.2 %collective-permute-start.4 = (bf16[288,640]{1,0:T(8,128)(2,1)}, bf16[288,640]{1,0:T(8,128)(2,1)S(1)}, u32[]{:S(2)}, u32[]{:S(2)}) collective-permute-start(bf16[288,640]{1,0:T(8,128)(2,1)} %get-tuple-element.18), channel_id=1, source_target_pairs={{0,5},{1,4},{2,7},{3,6},{4,1},{5,0},{6,3},{7,2},{8,13},{9,12},{10,... | collective-permute-start | bytes 1105928 | tf_op jit(solution)/shard_map/ppermute | solution.py:136
  78.9 31.7 %copy-start = (bf16[288,640]{1,0:T(8,128)(2,1)}, bf16[288,640]{1,0:T(8,128)(2,1)S(1)}, u32[]{:S(2)}) copy-start(bf16[288,640]{1,0:T(8,128)(2,1)S(1)} %collective-permute-done.refs_1_) | copy-start | bytes 1105924
  79.0 24.8 %collective-permute-start.5 = (bf16[288,640]{1,0:T(8,128)(2,1)}, bf16[288,640]{1,0:T(8,128)(2,1)S(1)}, u32[]{:S(2)}, u32[]{:S(2)}) collective-permute-start(bf16[288,640]{1,0:T(8,128)(2,1)} %get-tuple-element.19), channel_id=1, source_target_pairs={{0,6},{1,7},{2,4},{3,5},{4,2},{5,3},{6,0},{7,1},{8,14},{9,15},{10,... | collective-permute-start | bytes 1105928 | tf_op jit(solution)/shard_map/ppermute | solution.py:136
  83.4 27.2 %copy-start.1 = (bf16[288,640]{1,0:T(8,128)(2,1)}, bf16[288,640]{1,0:T(8,128)(2,1)S(1)}, u32[]{:S(2)}) copy-start(bf16[288,640]{1,0:T(8,128)(2,1)S(1)} %collective-permute-done.1.refs_2_) | copy-start | bytes 1105924
  83.4 27.2 %collective-permute-start.6 = (bf16[288,640]{1,0:T(8,128)(2,1)}, bf16[288,640]{1,0:T(8,128)(2,1)}, u32[]{:S(2)}, u32[]{:S(2)}) collective-permute-start(bf16[288,640]{1,0:T(8,128)(2,1)} %get-tuple-element.20), channel_id=1, source_target_pairs={{0,7},{1,6},{2,5},{3,4},{4,3},{5,2},{6,1},{7,0},{8,15},{9,14},{10,... | collective-permute-start | bytes 1105928 | tf_op jit(solution)/shard_map/ppermute | solution.py:136
  90.3 20.4 %copy-start.2 = (bf16[288,640]{1,0:T(8,128)(2,1)}, bf16[288,640]{1,0:T(8,128)(2,1)S(1)}, u32[]{:S(2)}) copy-start(bf16[288,640]{1,0:T(8,128)(2,1)S(1)} %collective-permute-done.2.refs_3_) | copy-start | bytes 1105924
  90.3 20.4 %copy-start.3 = (bf16[288,640]{1,0:T(8,128)(2,1)}, bf16[288,640]{1,0:T(8,128)(2,1)S(1)}, u32[]{:S(2)}) copy-start(bf16[288,640]{1,0:T(8,128)(2,1)S(1)} %collective-permute-done.3.refs_4_) | copy-start | bytes 1105924
  94.1 16.6 %copy-start.4 = (bf16[288,640]{1,0:T(8,128)(2,1)}, bf16[288,640]{1,0:T(8,128)(2,1)S(1)}, u32[]{:S(2)}) copy-start(bf16[288,640]{1,0:T(8,128)(2,1)S(1)} %collective-permute-done.4.refs_5_) | copy-start | bytes 1105924
  103.8 6.9 %copy-start.5 = (bf16[288,640]{1,0:T(8,128)(2,1)}, bf16[288,640]{1,0:T(8,128)(2,1)S(1)}, u32[]{:S(2)}) copy-start(bf16[288,640]{1,0:T(8,128)(2,1)S(1)} %collective-permute-done.5.refs_6_) | copy-start | bytes 1105924
  153.5 24.7 %all-to-all-start.3 = ((bf16[32,3,4,640]{3,2,1,0:T(4,128)(2,1)}), bf16[32,3,4,640]{3,2,1,0:T(4,128)(2,1)S(1)}, u32[]{:S(2)}, u32[]{:S(2)}) async-start(bf16[32,3,4,640]{3,2,1,0:T(4,128)(2,1)} %reshape.81), calls=%async_computation.3 | async-start | bytes 983040 | tf_op jit(solution)/shard_map/all_to_all | solution.py:15
  178.8 5.7 %copy-start.6 = (s32[4,3]{1,0:T(4,128)S(1)}, s32[4,3]{1,0:T(4,128)}, u32[]{:S(2)}) copy-start(s32[4,3]{1,0:T(4,128)} %param.8) | copy-start | bytes 148
  179.9 26.5 %all-to-all-start.4 = ((bf16[32,2,5120]{2,1,0:T(2,128)(2,1)}), bf16[32,2,5120]{2,1,0:T(2,128)(2,1)S(1)}, u32[]{:S(2)}, u32[]{:S(2)}) async-start(bf16[32,2,5120]{2,1,0:T(2,128)(2,1)} %reshape.84), calls=%async_computation.4 | async-start | bytes 1310720 | tf_op jit(solution)/shard_map/all_to_all | solution.py:15

commit v2 on v1

--- a/solution.py
+++ b/solution.py
@@ -9,6 +9,8 @@
 
 EXP_NODE = 4
 ALL = ("node", "e", "s")
+FIRST = (6, 4, 2, 7)
+THEN = (5, 3, 1)
 
 
 def swap(a, axis):
@@ -62,14 +64,26 @@
 
 
 def act_kernel(order, rows, *refs):
-    blocks, out = refs[:-1], refs[-1]
-    weights = jnp.concatenate([block[...] for block in blocks], axis=0)
-    made = lax.dot_general(
-        weights, rows[...], (((1,), (1,)), ((), ())), preferred_element_type=jnp.float32
-    ).astype(jnp.bfloat16)
-    size = blocks[0].shape[0]
-    for k in range(len(blocks)):
-        out[order[k]] = made[k * size : (k + 1) * size]
+    blocks, (out, hold, sem) = refs[:-3], refs[-3:]
+    parts, size = out.shape[:2]
+    reads = []
+    for k in range(parts):
+        target = hold.at[pl.ds(k * size, size), :]
+        reads.append(pltpu.make_async_copy(blocks[k].at[pl.ds(0, size), :], target, sem.at[k]))
+    for read in reads:
+        read.start()
+    half = parts // 2
+    for low in range(0, parts, half):
+        for read in reads[low : low + half]:
+            read.wait()
+        made = lax.dot_general(
+            hold[low * size : (low + half) * size],
+            rows[...],
+            (((1,), (1,)), ((), ())),
+            preferred_element_type=jnp.float32,
+        ).astype(jnp.bfloat16)
+        for k in range(half):
+            out[order[low + k]] = made[k * size : (k + 1) * size]
 
 
 def partial_acts(order, rows, blocks):
@@ -78,14 +92,17 @@
     parts = len(blocks)
     return pl.pallas_call(
         act_kernel,
-        grid=(1,),
         in_specs=[
             pl.BlockSpec(memory_space=pltpu.SMEM),
-            pl.BlockSpec((all_rows, width), lambda i: (0, 0)),
+            pl.BlockSpec(memory_space=pltpu.VMEM),
         ]
-        + [pl.BlockSpec((size, width), lambda i: (0, 0))] * parts,
-        out_specs=pl.BlockSpec((parts, size, all_rows), lambda i: (0, 0, 0)),
+        + [pl.BlockSpec(memory_space=pl.ANY)] * parts,
+        out_specs=pl.BlockSpec(memory_space=pltpu.VMEM),
         out_shape=jax.ShapeDtypeStruct((parts, size, all_rows), jnp.bfloat16),
+        scratch_shapes=[
+            pltpu.VMEM((parts * size, width), jnp.bfloat16),
+            pltpu.SemaphoreType.DMA((parts,)),
+        ],
         name="partial_acts",
     )(order, rows, *blocks)
 
@@ -131,9 +148,10 @@
 
     order = jnp.arange(slices, dtype=jnp.int32) ^ lax.axis_index("s").astype(jnp.int32)
     cut = cut_weights(order, w_gate, w_up, w_down, slices)
-    blocks = [cut[0]]
-    for k in range(1, slices):
-        blocks.append(lax.ppermute(cut[k], "s", [(a, a ^ k) for a in range(slices)]))
+    blocks = list(cut)
+    for steps in (FIRST, THEN):
+        for k in steps:
+            blocks[k] = lax.ppermute(cut[k], "s", [(a, a ^ k) for a in range(slices)])
 
     dest_node = node_pick.reshape(slot_count)
     slot_order = jnp.arange(slot_count, dtype=jnp.int32)
@@ -143,7 +161,9 @@
     slot_rank = jnp.sum(earlier.astype(jnp.int32), axis=1)
     position = dest_node * node_cap + slot_rank
     place = jnp.arange(node_slots, dtype=jnp.int32)[:, None] == position[None, :]
-    home = jnp.sum(place.reshape(node_slots, tok_rows, 3).astype(jnp.bfloat16), axis=2)
+    by_token = place.reshape(node_slots, tok_rows, 3).astype(jnp.bfloat16)
+    home = lax.optimization_barrier(by_token[..., 0] + by_token[..., 1])
+    home = lax.optimization_barrier(home + by_token[..., 2])
     local_pick = expert_pick.reshape(tok_rows, 3, 2)
     weights = gate_weight.reshape(tok_rows, 3, 2).astype(jnp.float32)
     chosen = (local_pick[..., None] == jnp.arange(EXP_NODE, dtype=jnp.int32)).astype(jnp.float32)

time: 208 us -> 209 us (level)
  no operation moved by 1% of the time
where the time goes in v2:
time: 209 us; the launch traced here: 208 us
  waiting for transfers between devices  86.1 us (41%)
  starting transfers between devices  62.7 us (30%)
  blocking collectives  33.7 us (16%)
  Pallas kernels  11.6 us (6%)
  local copies, waits for them, and re-layouts  10.9 us (5%)
    all_to_all x4, waiting for transfers between devices, swap(): return lax.all_to_all(a, axis, split_axis=0, concat_axis=0, tiled=True)  62.1 us
    all_to_all x4, starting transfers between devices, swap(): return lax.all_to_all(a, axis, split_axis=0, concat_axis=0, tiled=True)  42.7 us
    ppermute x7, waiting for transfers between devices, on_device(): blocks[k] = lax.ppermute(cut[k], 's', [(a, a ^ k) for a in range(slices)])  24 us
    all_to_all x1, blocking collectives, swap(): return lax.all_to_all(a, axis, split_axis=0, concat_axis=0, tiled=True)  20 us
    ppermute x7, starting transfers between devices, on_device(): blocks[k] = lax.ppermute(cut[k], 's', [(a, a ^ k) for a in range(slices)])  20 us
    all_gather x1, blocking collectives, on_device(): hidden = lax.all_gather(hidden, 's', axis=0)  13.7 us
    pallas_call x1, Pallas kernels, partial_acts(): pl.pallas_call(act_kernel, in_specs=[pl.BlockSpec(memory_space=pltpu.SMEM...  5.08 us
  transfers between devices with their start and end apart: 11, of which 7 were waited for; matrix products, arithmetic and copies ran while one was open for 1% of the time, Pallas kernels for 2%

profile of v2, /device:TPU:16, one launch (start us, length us, event | category | flops | bytes accessed | tf_op | source)
XLA Modules:
  0.0 208.5 jit_solution(14376874008593250991)
XLA Ops:
  0.0 0.8 eq.71
  0.8 0.2 convert_reduce_fusion.1
  1.0 0.8 copy.44
  1.7 0.8 copy.45
  2.5 0.1 select_reduce_fusion
  2.6 0.8 broadcast_in_dim.4
  3.5 0.1 reshape.75
  3.6 0.3 convolution_convert_fusion
  3.9 1.1 reshape.76
  5.0 22.0 %all-to-all-start = ((bf16[32,2,5124]{2,1,0:T(2,128)(2,1)}), bf16[32,2,5124]{2,1,0:T(2,128)(2,1)S(1)}, u32[]{:S(2)}, u32[]{:S(2)}) async-start(bf16[32,2,5124]{2,1,0:T(2,128)(2,1)} %reshape.76), calls=%async_computation | async-start | bytes 1343488 | tf_op jit(solution)/shard_map/all_to_all | solution.py:17
  27.0 0.1 eq.87
  27.1 23.3 %all-to-all-done = bf16[32,2,5124]{2,1,0:T(2,128)(2,1)S(1)} async-done(((bf16[32,2,5124]{2,1,0:T(2,128)(2,1)}), bf16[32,2,5124]{2,1,0:T(2,128)(2,1)S(1)}, u32[]{:S(2)}, u32[]{:S(2)}) %all-to-all-start) | async-done | bytes 655904 | tf_op jit(solution)/shard_map/all_to_all | solution.py:17
  50.4 0.5 reshape.77
  50.9 0.1 reduce_window_sum.11
  51.0 0.1 copy.49
  51.1 0.1 copy.48
  51.3 0.1 compare_and_fusion
  51.4 0.3 convolution_convert_fusion.2
  51.6 0.1 copy.56
  51.7 1.0 copy.51
  52.7 8.8 %all-to-all-start.1 = ((bf16[32,3,4,640]{3,2,1,0:T(4,128)(2,1)}), bf16[32,3,4,640]{3,2,1,0:T(4,128)(2,1)S(1)}, u32[]{:S(2)}, u32[]{:S(2)}) async-start(bf16[32,3,4,640]{3,2,1,0:T(4,128)(2,1)} %bitcast.6), calls=%async_computation.1 | async-start | bytes 983040 | tf_op jit(solution)/shard_map/all_to_all | solution.py:17
  61.4 0.5 iota_xor_fusion.order
  62.0 3.6 %cut_weights.1 = (bf16[288,640]{1,0:T(8,128)(2,1)}, bf16[288,640]{1,0:T(8,128)(2,1)}, bf16[288,640]{1,0:T(8,128)(2,1)}, bf16[288,640]{1,0:T(8,128)(2,1)}, bf16[2...) custom-call(s32[8]{0:T(128)} %iota_xor_fusion.order, ...), custom_call_target="tpu_custom_call" | custom-call | tf_op jit(solution)/shard_map/cut_weights/pallas_call | solution.py:52
  65.6 2.2 %collective-permute-start = (bf16[288,640]{1,0:T(8,128)(2,1)}, bf16[288,640]{1,0:T(8,128)(2,1)S(1)}, u32[]{:S(2)}, u32[]{:S(2)}) collective-permute-start(bf16[288,640]{1,0:T(8,128)(2,1)} %get-tuple-element.14), channel_id=1, source_target_pairs={{0,1},{1,0},{2,3},{3,2},{4,5},{5,4},{6,7},{7,6},{8,9},{9,8},{10,11... | collective-permute-start | bytes 1105928 | tf_op jit(solution)/shard_map/ppermute | solution.py:154
  67.8 3.5 %collective-permute-start.1 = (bf16[288,640]{1,0:T(8,128)(2,1)}, bf16[288,640]{1,0:T(8,128)(2,1)S(1)}, u32[]{:S(2)}, u32[]{:S(2)}) collective-permute-start(bf16[288,640]{1,0:T(8,128)(2,1)} %get-tuple-element.15), channel_id=1, source_target_pairs={{0,2},{1,3},{2,0},{3,1},{4,6},{5,7},{6,4},{7,5},{8,10},{9,11},{10,... | collective-permute-start | bytes 1105928 | tf_op jit(solution)/shard_map/ppermute | solution.py:154
  71.3 1.9 collective-permute-start.2
  73.3 3.6 %collective-permute-start.3 = (bf16[288,640]{1,0:T(8,128)(2,1)}, bf16[288,640]{1,0:T(8,128)(2,1)S(1)}, u32[]{:S(2)}, u32[]{:S(2)}) collective-permute-start(bf16[288,640]{1,0:T(8,128)(2,1)} %get-tuple-element.17), channel_id=1, source_target_pairs={{0,4},{1,5},{2,6},{3,7},{4,0},{5,1},{6,2},{7,3},{8,12},{9,13},{10,... | collective-permute-start | bytes 1105928 | tf_op jit(solution)/shard_map/ppermute | solution.py:154
  76.9 2.0 collective-permute-start.4
  78.9 0.0 collective-permute-done.refs_1_
  79.0 4.4 %collective-permute-start.5 = (bf16[288,640]{1,0:T(8,128)(2,1)}, bf16[288,640]{1,0:T(8,128)(2,1)S(1)}, u32[]{:S(2)}, u32[]{:S(2)}) collective-permute-start(bf16[288,640]{1,0:T(8,128)(2,1)} %get-tuple-element.19), channel_id=1, source_target_pairs={{0,6},{1,7},{2,4},{3,5},{4,2},{5,3},{6,0},{7,1},{8,14},{9,15},{10,... | collective-permute-start | bytes 1105928 | tf_op jit(solution)/shard_map/ppermute | solution.py:154
  83.4 0.0 collective-permute-done.1.refs_2_
  83.4 2.3 %collective-permute-start.6 = (bf16[288,640]{1,0:T(8,128)(2,1)}, bf16[288,640]{1,0:T(8,128)(2,1)}, u32[]{:S(2)}, u32[]{:S(2)}) collective-permute-start(bf16[288,640]{1,0:T(8,128)(2,1)} %get-tuple-element.20), channel_id=1, source_target_pairs={{0,7},{1,6},{2,5},{3,4},{4,3},{5,2},{6,1},{7,0},{8,15},{9,14},{10,... | collective-permute-start | bytes 1105928 | tf_op jit(solution)/shard_map/ppermute | solution.py:154
  85.7 0.0 all-to-all-done.1
  85.7 0.9 reshape.81.rows
  86.6 3.6 %collective-permute-done.2.refs_3_ = bf16[288,640]{1,0:T(8,128)(2,1)S(1)} collective-permute-done((bf16[288,640]{1,0:T(8,128)(2,1)}, bf16[288,640]{1,0:T(8,128)(2,1)S(1)}, u32[]{:S(2)}, u32[]{:S(2)}) %collective-permute-start.2) | collective-permute-done | bytes 368672 | tf_op jit(solution)/shard_map/ppermute | solution.py:154
  90.3 0.0 collective-permute-done.3.refs_4_
  90.3 3.8 %collective-permute-done.4.refs_5_ = bf16[288,640]{1,0:T(8,128)(2,1)S(1)} collective-permute-done((bf16[288,640]{1,0:T(8,128)(2,1)}, bf16[288,640]{1,0:T(8,128)(2,1)S(1)}, u32[]{:S(2)}, u32[]{:S(2)}) %collective-permute-start.4) | collective-permute-done | bytes 368672 | tf_op jit(solution)/shard_map/ppermute | solution.py:154
  94.1 9.7 %collective-permute-done.5.refs_6_ = bf16[288,640]{1,0:T(8,128)(2,1)S(1)} collective-permute-done((bf16[288,640]{1,0:T(8,128)(2,1)}, bf16[288,640]{1,0:T(8,128)(2,1)S(1)}, u32[]{:S(2)}, u32[]{:S(2)}) %collective-permute-start.5) | collective-permute-done | bytes 368672 | tf_op jit(solution)/shard_map/ppermute | solution.py:154
  103.8 6.9 %collective-permute-done.6.refs_7_ = bf16[288,640]{1,0:T(8,128)(2,1)} collective-permute-done((bf16[288,640]{1,0:T(8,128)(2,1)}, bf16[288,640]{1,0:T(8,128)(2,1)}, u32[]{:S(2)}, u32[]{:S(2)}) %collective-permute-start.6) | collective-permute-done | bytes 368672 | tf_op jit(solution)/shard_map/ppermute | solution.py:154
  110.6 0.0 copy-done.2
  110.7 0.0 copy-done.3
  110.7 0.0 copy-done.4
  110.7 5.1 %partial_acts.1 = bf16[8,192,384]{2,1,0:T(8,128)(2,1)} custom-call(s32[8]{0:T(128)} %iota_xor_fusion.order, bf16[384,640]{1,0:T(8,128)(2,1)} %reshape.81.rows, bf16[288,640]{1,0:T(8,128)(2,1)} %get-tuple-element.13.refs_0_, bf16[288,640]{1,0:T(8,128)(2,1)} %copy-done, bf16[288,640]{1,0:T(8,128)(2,1)} %copy-done.1, bf16[288,640]{1,0:T(8,128)(2,1)} %copy-done.2, ...), custom_call_target="tpu_custom_call" | custom-call | tf_op jit(solution)/shard_map/partial_acts/pallas_call | solution.py:93
  115.8 20.0 %all_to_all.25 = bf16[8,192,384]{2,1,0:T(8,128)(2,1)S(1)} all-to-all(bf16[8,192,384]{2,1,0:T(8,128)(2,1)} %partial_acts.1), channel_id=1, replica_groups=mesh['node'=32,'e'=4,'s'=8] {'s'}, dimensions={0} | all-to-all | bytes 2359296 | tf_op jit(solution)/shard_map/all_to_all | solution.py:17
  135.8 0.2 convert_reduce_fusion
  136.0 0.1 fusion.4
  136.0 13.7 %all-gather = bf16[768,384]{1,0:T(8,128)(2,1)} all-gather(bf16[96,384]{1,0:T(8,128)(2,1)S(1)} %fusion.4), channel_id=2, replica_groups=mesh['node'=32,'e'=4,'s'=8] {'s'}, dimensions={0}, use_global_device_ids=true | all-gather | bytes 663552 | tf_op jit(solution)/shard_map/all_gather | solution.py:197
  149.7 2.9 %down_rows.1 = bf16[384,640]{1,0:T(8,128)(2,1)} custom-call(s32[8]{0:T(128)} %iota_xor_fusion.order, bf16[8,96,384]{2,1,0:T(8,128)(2,1)} %bitcast.36, bf16[288,640]{1,0:T(8,128)(2,1)} %get-tuple-element.13.refs_0_, bf16[288,640]{1,0:T(8,128)(2,1)} %copy-done, bf16[288,640]{1,0:T(8,128)(2,1)} %copy-done.1, bf16[288,640]{1,0:T(8,128)(2,1)} %copy-done.2, ...), custom_call_target="tpu_custom_call" | custom-call | tf_op jit(solution)/shard_map/down_rows/pallas_call | solution.py:122
  152.6 1.9 reshape.82
  154.5 7.4 %all-to-all-start.3 = ((bf16[32,3,4,640]{3,2,1,0:T(4,128)(2,1)}), bf16[32,3,4,640]{3,2,1,0:T(4,128)(2,1)S(1)}, u32[]{:S(2)}, u32[]{:S(2)}) async-start(bf16[32,3,4,640]{3,2,1,0:T(4,128)(2,1)} %reshape.82), calls=%async_computation.3 | async-start | bytes 983040 | tf_op jit(solution)/shard_map/all_to_all | solution.py:17
  162.0 0.1 copy.50
  162.1 17.2 %all-to-all-done.3 = bf16[32,3,4,640]{3,2,1,0:T(4,128)(2,1)S(1)} async-done(((bf16[32,3,4,640]{3,2,1,0:T(4,128)(2,1)}), bf16[32,3,4,640]{3,2,1,0:T(4,128)(2,1)S(1)}, u32[]{:S(2)}, u32[]{:S(2)}) %all-to-all-start.3) | async-done | bytes 491552 | tf_op jit(solution)/shard_map/all_to_all | solution.py:17
  179.2 0.1 copy.52
  179.4 0.1 copy.57
  179.4 0.4 convolution_convert_fusion.1
  179.8 0.0 copy-start.6
  179.8 1.1 reshape.85
  180.9 4.6 %all-to-all-start.4 = ((bf16[32,2,5120]{2,1,0:T(2,128)(2,1)}), bf16[32,2,5120]{2,1,0:T(2,128)(2,1)S(1)}, u32[]{:S(2)}, u32[]{:S(2)}) async-start(bf16[32,2,5120]{2,1,0:T(2,128)(2,1)} %reshape.85), calls=%async_computation.4 | async-start | bytes 1310720 | tf_op jit(solution)/shard_map/all_to_all | solution.py:17
  185.5 0.1 reduce_sum.30
  185.5 0.1 copy.43
  185.6 0.1 fusion.8
  185.7 21.6 %all-to-all-done.4 = bf16[32,2,5120]{2,1,0:T(2,128)(2,1)S(1)} async-done(((bf16[32,2,5120]{2,1,0:T(2,128)(2,1)}), bf16[32,2,5120]{2,1,0:T(2,128)(2,1)S(1)}, u32[]{:S(2)}, u32[]{:S(2)}) %all-to-all-start.4) | async-done | bytes 655392 | tf_op jit(solution)/shard_map/all_to_all | solution.py:17
  207.4 0.2 reshape.86
  207.6 0.8 convolution_convert_fusion.3
  (29 shorter events, 0.2 us)
Async XLA Ops:
  5.0 45.4 %all-to-all-start = ((bf16[32,2,5124]{2,1,0:T(2,128)(2,1)}), bf16[32,2,5124]{2,1,0:T(2,128)(2,1)S(1)}, u32[]{:S(2)}, u32[]{:S(2)}) async-start(bf16[32,2,5124]{2,1,0:T(2,128)(2,1)} %reshape.76), calls=%async_computation | async-start | bytes 1343488 | tf_op jit(solution)/shard_map/all_to_all | solution.py:17
  52.7 33.0 %all-to-all-start.1 = ((bf16[32,3,4,640]{3,2,1,0:T(4,128)(2,1)}), bf16[32,3,4,640]{3,2,1,0:T(4,128)(2,1)S(1)}, u32[]{:S(2)}, u32[]{:S(2)}) async-start(bf16[32,3,4,640]{3,2,1,0:T(4,128)(2,1)} %bitcast.6), calls=%async_computation.1 | async-start | bytes 983040 | tf_op jit(solution)/shard_map/all_to_all | solution.py:17
  65.6 13.3 %collective-permute-start = (bf16[288,640]{1,0:T(8,128)(2,1)}, bf16[288,640]{1,0:T(8,128)(2,1)S(1)}, u32[]{:S(2)}, u32[]{:S(2)}) collective-permute-start(bf16[288,640]{1,0:T(8,128)(2,1)} %get-tuple-element.14), channel_id=1, source_target_pairs={{0,1},{1,0},{2,3},{3,2},{4,5},{5,4},{6,7},{7,6},{8,9},{9,8},{10,11... | collective-permute-start | bytes 1105928 | tf_op jit(solution)/shard_map/ppermute | solution.py:154
  67.8 15.6 %collective-permute-start.1 = (bf16[288,640]{1,0:T(8,128)(2,1)}, bf16[288,640]{1,0:T(8,128)(2,1)S(1)}, u32[]{:S(2)}, u32[]{:S(2)}) collective-permute-start(bf16[288,640]{1,0:T(8,128)(2,1)} %get-tuple-element.15), channel_id=1, source_target_pairs={{0,2},{1,3},{2,0},{3,1},{4,6},{5,7},{6,4},{7,5},{8,10},{9,11},{10,... | collective-permute-start | bytes 1105928 | tf_op jit(solution)/shard_map/ppermute | solution.py:154
  71.3 19.0 %collective-permute-start.2 = (bf16[288,640]{1,0:T(8,128)(2,1)}, bf16[288,640]{1,0:T(8,128)(2,1)S(1)}, u32[]{:S(2)}, u32[]{:S(2)}) collective-permute-start(bf16[288,640]{1,0:T(8,128)(2,1)} %get-tuple-element.16), channel_id=1, source_target_pairs={{0,3},{1,2},{2,1},{3,0},{4,7},{5,6},{6,5},{7,4},{8,11},{9,10},{10,... | collective-permute-start | bytes 1105928 | tf_op jit(solution)/shard_map/ppermute | solution.py:154
  73.3 17.0 %collective-permute-start.3 = (bf16[288,640]{1,0:T(8,128)(2,1)}, bf16[288,640]{1,0:T(8,128)(2,1)S(1)}, u32[]{:S(2)}, u32[]{:S(2)}) collective-permute-start(bf16[288,640]{1,0:T(8,128)(2,1)} %get-tuple-element.17), channel_id=1, source_target_pairs={{0,4},{1,5},{2,6},{3,7},{4,0},{5,1},{6,2},{7,3},{8,12},{9,13},{10,... | collective-permute-start | bytes 1105928 | tf_op jit(solution)/shard_map/ppermute | solution.py:154
  76.9 17.2 %collective-permute-start.4 = (bf16[288,640]{1,0:T(8,128)(2,1)}, bf16[288,640]{1,0:T(8,128)(2,1)S(1)}, u32[]{:S(2)}, u32[]{:S(2)}) collective-permute-start(bf16[288,640]{1,0:T(8,128)(2,1)} %get-tuple-element.18), channel_id=1, source_target_pairs={{0,5},{1,4},{2,7},{3,6},{4,1},{5,0},{6,3},{7,2},{8,13},{9,12},{10,... | collective-permute-start | bytes 1105928 | tf_op jit(solution)/shard_map/ppermute | solution.py:154
  78.9 31.7 %copy-start = (bf16[288,640]{1,0:T(8,128)(2,1)}, bf16[288,640]{1,0:T(8,128)(2,1)S(1)}, u32[]{:S(2)}) copy-start(bf16[288,640]{1,0:T(8,128)(2,1)S(1)} %collective-permute-done.refs_1_) | copy-start | bytes 1105924
  79.0 24.8 %collective-permute-start.5 = (bf16[288,640]{1,0:T(8,128)(2,1)}, bf16[288,640]{1,0:T(8,128)(2,1)S(1)}, u32[]{:S(2)}, u32[]{:S(2)}) collective-permute-start(bf16[288,640]{1,0:T(8,128)(2,1)} %get-tuple-element.19), channel_id=1, source_target_pairs={{0,6},{1,7},{2,4},{3,5},{4,2},{5,3},{6,0},{7,1},{8,14},{9,15},{10,... | collective-permute-start | bytes 1105928 | tf_op jit(solution)/shard_map/ppermute | solution.py:154
  83.4 27.2 %copy-start.1 = (bf16[288,640]{1,0:T(8,128)(2,1)}, bf16[288,640]{1,0:T(8,128)(2,1)S(1)}, u32[]{:S(2)}) copy-start(bf16[288,640]{1,0:T(8,128)(2,1)S(1)} %collective-permute-done.1.refs_2_) | copy-start | bytes 1105924
  83.4 27.2 %collective-permute-start.6 = (bf16[288,640]{1,0:T(8,128)(2,1)}, bf16[288,640]{1,0:T(8,128)(2,1)}, u32[]{:S(2)}, u32[]{:S(2)}) collective-permute-start(bf16[288,640]{1,0:T(8,128)(2,1)} %get-tuple-element.20), channel_id=1, source_target_pairs={{0,7},{1,6},{2,5},{3,4},{4,3},{5,2},{6,1},{7,0},{8,15},{9,14},{10,... | collective-permute-start | bytes 1105928 | tf_op jit(solution)/shard_map/ppermute | solution.py:154
  90.3 20.4 %copy-start.2 = (bf16[288,640]{1,0:T(8,128)(2,1)}, bf16[288,640]{1,0:T(8,128)(2,1)S(1)}, u32[]{:S(2)}) copy-start(bf16[288,640]{1,0:T(8,128)(2,1)S(1)} %collective-permute-done.2.refs_3_) | copy-start | bytes 1105924
  90.3 20.4 %copy-start.3 = (bf16[288,640]{1,0:T(8,128)(2,1)}, bf16[288,640]{1,0:T(8,128)(2,1)S(1)}, u32[]{:S(2)}) copy-start(bf16[288,640]{1,0:T(8,128)(2,1)S(1)} %collective-permute-done.3.refs_4_) | copy-start | bytes 1105924
  94.1 16.6 %copy-start.4 = (bf16[288,640]{1,0:T(8,128)(2,1)}, bf16[288,640]{1,0:T(8,128)(2,1)S(1)}, u32[]{:S(2)}) copy-start(bf16[288,640]{1,0:T(8,128)(2,1)S(1)} %collective-permute-done.4.refs_5_) | copy-start | bytes 1105924
  103.8 6.9 %copy-start.5 = (bf16[288,640]{1,0:T(8,128)(2,1)}, bf16[288,640]{1,0:T(8,128)(2,1)S(1)}, u32[]{:S(2)}) copy-start(bf16[288,640]{1,0:T(8,128)(2,1)S(1)} %collective-permute-done.5.refs_6_) | copy-start | bytes 1105924
  154.5 24.7 %all-to-all-start.3 = ((bf16[32,3,4,640]{3,2,1,0:T(4,128)(2,1)}), bf16[32,3,4,640]{3,2,1,0:T(4,128)(2,1)S(1)}, u32[]{:S(2)}, u32[]{:S(2)}) async-start(bf16[32,3,4,640]{3,2,1,0:T(4,128)(2,1)} %reshape.82), calls=%async_computation.3 | async-start | bytes 983040 | tf_op jit(solution)/shard_map/all_to_all | solution.py:17
  179.8 5.8 %copy-start.6 = (s32[4,3]{1,0:T(4,128)S(1)}, s32[4,3]{1,0:T(4,128)}, u32[]{:S(2)}) copy-start(s32[4,3]{1,0:T(4,128)} %param.8) | copy-start | bytes 148
  180.9 26.5 %all-to-all-start.4 = ((bf16[32,2,5120]{2,1,0:T(2,128)(2,1)}), bf16[32,2,5120]{2,1,0:T(2,128)(2,1)S(1)}, u32[]{:S(2)}, u32[]{:S(2)}) async-start(bf16[32,2,5120]{2,1,0:T(2,128)(2,1)} %reshape.85), calls=%async_computation.4 | async-start | bytes 1310720 | tf_op jit(solution)/shard_map/all_to_all | solution.py:17

commit v3 on v1

--- a/solution.py
+++ b/solution.py
@@ -8,7 +8,11 @@
 
 
 EXP_NODE = 4
-ALL = ("node", "e", "s")
+ALL = ("node", "e", "q", "c")
+PART = ("q", "c")
+STEPS = (0, 6, 4, 2, 7, 5, 3, 1)
+FIRST = (1, 2, 3, 4)
+THEN = (5, 6, 7)
 
 
 def swap(a, axis):
@@ -78,47 +82,50 @@
     parts = len(blocks)
     return pl.pallas_call(
         act_kernel,
-        grid=(1,),
+        grid=(all_rows // 128,),
         in_specs=[
             pl.BlockSpec(memory_space=pltpu.SMEM),
-            pl.BlockSpec((all_rows, width), lambda i: (0, 0)),
+            pl.BlockSpec((128, width), lambda i: (i, 0)),
         ]
         + [pl.BlockSpec((size, width), lambda i: (0, 0))] * parts,
-        out_specs=pl.BlockSpec((parts, size, all_rows), lambda i: (0, 0, 0)),
+        out_specs=pl.BlockSpec((parts, size, 128), lambda i: (0, 0, i)),
         out_shape=jax.ShapeDtypeStruct((parts, size, all_rows), jnp.bfloat16),
         name="partial_acts",
     )(order, rows, *blocks)
 
 
-def down_kernel(order, hidden, *refs):
+def down_kernel(order, mine, other, *refs):
     blocks, out = refs[:-1], refs[-1]
     weights = jnp.concatenate([block[...] for block in blocks], axis=0)
-    units = jnp.concatenate([hidden[order[k]] for k in range(len(blocks))], axis=0)
+    held = [other if STEPS[k] % 2 else mine for k in range(len(blocks))]
+    units = jnp.concatenate([held[k][order[k] // 2] for k in range(len(blocks))], axis=0)
     out[...] = lax.dot_general(
         units, weights, (((0,), (0,)), ((), ())), preferred_element_type=jnp.float32
     ).astype(jnp.bfloat16)
 
 
-def down_rows(order, hidden, blocks):
-    parts, size, all_rows = hidden.shape
+def down_rows(order, mine, other, blocks):
+    chips, size, all_rows = mine.shape
+    parts = len(blocks)
     width = blocks[0].shape[1]
     return pl.pallas_call(
         down_kernel,
         grid=(1,),
         in_specs=[
             pl.BlockSpec(memory_space=pltpu.SMEM),
-            pl.BlockSpec((parts, size, all_rows), lambda i: (0, 0, 0)),
+            pl.BlockSpec((chips, size, all_rows), lambda i: (0, 0, 0)),
+            pl.BlockSpec((chips, size, all_rows), lambda i: (0, 0, 0)),
         ]
         + [pl.BlockSpec((size, width), lambda i: (2, 0))] * parts,
         out_specs=pl.BlockSpec((all_rows, width), lambda i: (0, 0)),
         out_shape=jax.ShapeDtypeStruct((all_rows, width), jnp.bfloat16),
         name="down_rows",
-    )(order, hidden, *blocks)
+    )(order, mine, other, *blocks)
 
 
 def on_device(tokens, node_pick, expert_pick, gate_weight, w_gate, w_up, w_down):
     node_count = lax.axis_size("node")
-    slices = lax.axis_size("s")
+    slices = lax.axis_size(PART)
     dev_count = EXP_NODE * slices
     tok_rows, feature_dim = tokens.shape
     width = feature_dim // slices
@@ -129,11 +136,13 @@
     hidden_rows = w_gate.shape[0]
     all_rows = dev_count * slot_count
 
-    order = jnp.arange(slices, dtype=jnp.int32) ^ lax.axis_index("s").astype(jnp.int32)
+    order = jnp.array(STEPS, jnp.int32) ^ lax.axis_index(PART).astype(jnp.int32)
     cut = cut_weights(order, w_gate, w_up, w_down, slices)
-    blocks = [cut[0]]
-    for k in range(1, slices):
-        blocks.append(lax.ppermute(cut[k], "s", [(a, a ^ k) for a in range(slices)]))
+    blocks = list(cut)
+    for steps in (FIRST, THEN):
+        for k in steps:
+            pairs = [(a, a ^ STEPS[k]) for a in range(slices)]
+            blocks[k] = lax.ppermute(cut[k], PART, pairs)
 
     dest_node = node_pick.reshape(slot_count)
     slot_order = jnp.arange(slot_count, dtype=jnp.int32)
@@ -143,7 +152,9 @@
     slot_rank = jnp.sum(earlier.astype(jnp.int32), axis=1)
     position = dest_node * node_cap + slot_rank
     place = jnp.arange(node_slots, dtype=jnp.int32)[:, None] == position[None, :]
-    home = jnp.sum(place.reshape(node_slots, tok_rows, 3).astype(jnp.bfloat16), axis=2)
+    by_token = place.reshape(node_slots, tok_rows, 3).astype(jnp.bfloat16)
+    home = lax.optimization_barrier(by_token[..., 0] + by_token[..., 1])
+    home = lax.optimization_barrier(home + by_token[..., 2])
     local_pick = expert_pick.reshape(tok_rows, 3, 2)
     weights = gate_weight.reshape(tok_rows, 3, 2).astype(jnp.float32)
     chosen = (local_pick[..., None] == jnp.arange(EXP_NODE, dtype=jnp.int32)).astype(jnp.float32)
@@ -167,16 +178,17 @@
     ).astype(jnp.bfloat16)
     quads = slot_count // 4
     outgoing = packed.reshape(EXP_NODE, quads, 4, slices, width).transpose(0, 3, 1, 2, 4)
-    arrived = swap(outgoing.reshape(dev_count, quads, 4, width), ("e", "s"))
+    arrived = swap(outgoing.reshape(dev_count, quads, 4, width), ("e", *PART))
     rows = arrived.reshape(all_rows, width)
 
     acts = partial_acts(order, rows, blocks)
-    acts = swap(acts, "s")
+    acts = swap(acts, PART)
     acts = jnp.sum(acts.astype(jnp.float32), axis=0)
     hidden = (jax.nn.silu(acts[:hidden_rows]) * acts[hidden_rows:]).astype(jnp.bfloat16)
-    hidden = lax.all_gather(hidden, "s", axis=0)
-    made = down_rows(order, hidden, blocks)
-    returned = swap(made.reshape(dev_count, quads, 4, width), ("e", "s"))
+    mine = lax.all_gather(hidden, "q", axis=0)
+    other = lax.ppermute(mine, "c", [(0, 1), (1, 0)])
+    made = down_rows(order, mine, other, blocks)
+    returned = swap(made.reshape(dev_count, quads, 4, width), ("e", *PART))
     expert_out = returned.reshape(EXP_NODE, slices, slot_count, width).transpose(0, 2, 1, 3)
     expert_out = expert_out.reshape(EXP_NODE * slot_count, feature_dim)
     combine = pick_table.T.astype(jnp.bfloat16) * jnp.repeat(got_meta, slot_count, axis=1)
@@ -188,6 +200,6 @@
 
 def solution(mesh):
     slices = mesh.shape["dev"] // EXP_NODE
-    fine = Mesh(mesh.devices.reshape(mesh.shape["node"], EXP_NODE, slices), ALL)
+    fine = Mesh(mesh.devices.reshape(mesh.shape["node"], EXP_NODE, slices // 2, 2), ALL)
     spec = P(ALL, None)
     return jax.shard_map(on_device, mesh=fine, in_specs=(spec,) * 7, out_specs=spec, check_vma=False)

time: 208 us -> 208 us (level)
    ppermute x7 -> x8, starting transfers between devices: 20 us -> 21.7 us  [the longest x7 19.8 us: on_device(): blocks[k] = lax.ppermute(cut[k], PART, pairs)]
    ppermute x7 -> x8, waiting for transfers between devices: 24 us -> 22.5 us  [the longest x7 21 us: on_device(): blocks[k] = lax.ppermute(cut[k], PART, pairs)]
  transfers between devices with their start and end apart: 11 -> 12, of which waited for: 7 -> 9; matrix products, arithmetic and copies ran while one was open for 1% -> 1% of each run, Pallas kernels for 2% -> 2%
where the time goes in v3:
time: 208 us; the launch traced here: 207 us
  waiting for transfers between devices  84.6 us (41%)
  starting transfers between devices  63.3 us (30%)
  blocking collectives  32.2 us (15%)
  local copies, waits for them, and re-layouts  12.3 us (6%)
  Pallas kernels  11.4 us (5%)
    all_to_all x4, waiting for transfers between devices, swap(): return lax.all_to_all(a, axis, split_axis=0, concat_axis=0, tiled=True)  62.1 us
    all_to_all x4, starting transfers between devices, swap(): return lax.all_to_all(a, axis, split_axis=0, concat_axis=0, tiled=True)  41.6 us
    ppermute x7, waiting for transfers between devices, on_device(): blocks[k] = lax.ppermute(cut[k], PART, pairs)  21 us
    all_to_all x1, blocking collectives, swap(): return lax.all_to_all(a, axis, split_axis=0, concat_axis=0, tiled=True)  20 us
    ppermute x7, starting transfers between devices, on_device(): blocks[k] = lax.ppermute(cut[k], PART, pairs)  19.8 us
    all_gather x1, blocking collectives, on_device(): mine = lax.all_gather(hidden, 'q', axis=0)  12.2 us
    pallas_call x1, Pallas kernels, partial_acts(): pl.pallas_call(act_kernel, grid=(all_rows // 128,), in_specs=[pl.BlockSpe...  4.88 us
  transfers between devices with their start and end apart: 12, of which 9 were waited for; matrix products, arithmetic and copies ran while one was open for 1% of the time, Pallas kernels for 2%

profile of v3, /device:TPU:16, one launch (start us, length us, event | category | flops | bytes accessed | tf_op | source)
XLA Modules:
  0.0 207.2 jit_solution(8658448928657635665)
XLA Ops:
  0.0 0.8 eq.71
  0.8 0.2 convert_reduce_fusion.1
  1.0 0.8 copy.45
  1.7 0.8 copy.46
  2.5 0.1 select_reduce_fusion
  2.6 0.8 broadcast_in_dim.4
  3.5 0.1 reshape.75
  3.6 0.3 convolution_convert_fusion
  3.9 1.1 reshape.76
  5.0 22.0 %all-to-all-start = ((bf16[32,2,5124]{2,1,0:T(2,128)(2,1)}), bf16[32,2,5124]{2,1,0:T(2,128)(2,1)S(1)}, u32[]{:S(2)}, u32[]{:S(2)}) async-start(bf16[32,2,5124]{2,1,0:T(2,128)(2,1)} %reshape.76), calls=%async_computation | async-start | bytes 1343488 | tf_op jit(solution)/shard_map/all_to_all | solution.py:19
  27.0 0.1 eq.87
  27.1 23.3 %all-to-all-done = bf16[32,2,5124]{2,1,0:T(2,128)(2,1)S(1)} async-done(((bf16[32,2,5124]{2,1,0:T(2,128)(2,1)}), bf16[32,2,5124]{2,1,0:T(2,128)(2,1)S(1)}, u32[]{:S(2)}, u32[]{:S(2)}) %all-to-all-start) | async-done | bytes 655904 | tf_op jit(solution)/shard_map/all_to_all | solution.py:19
  50.4 0.5 reshape.77
  50.9 0.1 reduce_window_sum.11
  51.0 0.1 copy.50
  51.1 0.1 copy.49
  51.3 0.1 compare_and_fusion
  51.3 0.3 convolution_convert_fusion.2
  51.6 0.1 copy.57
  51.7 0.0 copy-start.9
  51.7 1.0 copy.52
  52.7 8.8 %all-to-all-start.1 = ((bf16[32,3,4,640]{3,2,1,0:T(4,128)(2,1)}), bf16[32,3,4,640]{3,2,1,0:T(4,128)(2,1)S(1)}, u32[]{:S(2)}, u32[]{:S(2)}) async-start(bf16[32,3,4,640]{3,2,1,0:T(4,128)(2,1)} %bitcast.6), calls=%async_computation.1 | async-start | bytes 983040 | tf_op jit(solution)/shard_map/all_to_all | solution.py:19
  61.4 0.5 broadcast_xor_fusion.order
  62.0 3.6 %cut_weights.1 = (bf16[288,640]{1,0:T(8,128)(2,1)}, bf16[288,640]{1,0:T(8,128)(2,1)}, bf16[288,640]{1,0:T(8,128)(2,1)}, bf16[288,640]{1,0:T(8,128)(2,1)}, bf16[2...) custom-call(s32[8]{0:T(128)} %broadcast_xor_fusion.order, ...), custom_call_target="tpu_custom_call" | custom-call | tf_op jit(solution)/shard_map/cut_weights/pallas_call | solution.py:54
  65.6 4.6 %collective-permute-start = (bf16[288,640]{1,0:T(8,128)(2,1)}, bf16[288,640]{1,0:T(8,128)(2,1)S(1)}, u32[]{:S(2)}, u32[]{:S(2)}) collective-permute-start(bf16[288,640]{1,0:T(8,128)(2,1)} %get-tuple-element.14), channel_id=1, source_target_pairs={{0,6},{1,7},{2,4},{3,5},{4,2},{5,3},{6,0},{7,1},{8,14},{9,15},{10,... | collective-permute-start | bytes 1105928 | tf_op jit(solution)/shard_map/ppermute | solution.py:145
  70.2 2.5 %collective-permute-start.1 = (bf16[288,640]{1,0:T(8,128)(2,1)}, bf16[288,640]{1,0:T(8,128)(2,1)S(1)}, u32[]{:S(2)}, u32[]{:S(2)}) collective-permute-start(bf16[288,640]{1,0:T(8,128)(2,1)} %get-tuple-element.15), channel_id=1, source_target_pairs={{0,4},{1,5},{2,6},{3,7},{4,0},{5,1},{6,2},{7,3},{8,12},{9,13},{10,... | collective-permute-start | bytes 1105928 | tf_op jit(solution)/shard_map/ppermute | solution.py:145
  72.7 2.1 %collective-permute-start.2 = (bf16[288,640]{1,0:T(8,128)(2,1)}, bf16[288,640]{1,0:T(8,128)(2,1)S(1)}, u32[]{:S(2)}, u32[]{:S(2)}) collective-permute-start(bf16[288,640]{1,0:T(8,128)(2,1)} %get-tuple-element.16), channel_id=1, source_target_pairs={{0,2},{1,3},{2,0},{3,1},{4,6},{5,7},{6,4},{7,5},{8,10},{9,11},{10,... | collective-permute-start | bytes 1105928 | tf_op jit(solution)/shard_map/ppermute | solution.py:145
  74.8 3.5 %collective-permute-start.3 = (bf16[288,640]{1,0:T(8,128)(2,1)}, bf16[288,640]{1,0:T(8,128)(2,1)S(1)}, u32[]{:S(2)}, u32[]{:S(2)}) collective-permute-start(bf16[288,640]{1,0:T(8,128)(2,1)} %get-tuple-element.17), channel_id=1, source_target_pairs={{0,7},{1,6},{2,5},{3,4},{4,3},{5,2},{6,1},{7,0},{8,15},{9,14},{10,... | collective-permute-start | bytes 1105928 | tf_op jit(solution)/shard_map/ppermute | solution.py:145
  78.3 3.3 %collective-permute-start.4 = (bf16[288,640]{1,0:T(8,128)(2,1)}, bf16[288,640]{1,0:T(8,128)(2,1)S(1)}, u32[]{:S(2)}, u32[]{:S(2)}) collective-permute-start(bf16[288,640]{1,0:T(8,128)(2,1)} %get-tuple-element.18), channel_id=1, source_target_pairs={{0,5},{1,4},{2,7},{3,6},{4,1},{5,0},{6,3},{7,2},{8,13},{9,12},{10,... | collective-permute-start | bytes 1105928 | tf_op jit(solution)/shard_map/ppermute | solution.py:145
  81.6 2.7 %collective-permute-done.refs_1_ = bf16[288,640]{1,0:T(8,128)(2,1)S(1)} collective-permute-done((bf16[288,640]{1,0:T(8,128)(2,1)}, bf16[288,640]{1,0:T(8,128)(2,1)S(1)}, u32[]{:S(2)}, u32[]{:S(2)}) %collective-permute-start) | collective-permute-done | bytes 368672 | tf_op jit(solution)/shard_map/ppermute | solution.py:145
  84.4 1.9 collective-permute-start.5
  86.3 5.1 %collective-permute-done.1.refs_2_ = bf16[288,640]{1,0:T(8,128)(2,1)S(1)} collective-permute-done((bf16[288,640]{1,0:T(8,128)(2,1)}, bf16[288,640]{1,0:T(8,128)(2,1)S(1)}, u32[]{:S(2)}, u32[]{:S(2)}) %collective-permute-start.1) | collective-permute-done | bytes 368672 | tf_op jit(solution)/shard_map/ppermute | solution.py:145
  91.4 1.9 collective-permute-start.6
  93.3 0.9 reshape.81.rows
  94.2 4.9 %collective-permute-done.3.refs_4_ = bf16[288,640]{1,0:T(8,128)(2,1)S(1)} collective-permute-done((bf16[288,640]{1,0:T(8,128)(2,1)}, bf16[288,640]{1,0:T(8,128)(2,1)S(1)}, u32[]{:S(2)}, u32[]{:S(2)}) %collective-permute-start.3) | collective-permute-done | bytes 368672 | tf_op jit(solution)/shard_map/ppermute | solution.py:145
  99.1 7.0 %collective-permute-done.4.refs_5_ = bf16[288,640]{1,0:T(8,128)(2,1)S(1)} collective-permute-done((bf16[288,640]{1,0:T(8,128)(2,1)}, bf16[288,640]{1,0:T(8,128)(2,1)S(1)}, u32[]{:S(2)}, u32[]{:S(2)}) %collective-permute-start.4) | collective-permute-done | bytes 368672 | tf_op jit(solution)/shard_map/ppermute | solution.py:145
  106.1 1.3 collective-permute-done.5.refs_6_
  107.4 0.0 collective-permute-done.6.refs_7_
  107.4 0.7 copy-done.5
  108.1 4.9 %partial_acts.1 = bf16[8,192,384]{2,1,0:T(8,128)(2,1)} custom-call(s32[8]{0:T(128)} %broadcast_xor_fusion.order, bf16[384,640]{1,0:T(8,128)(2,1)} %reshape.81.rows, bf16[288,640]{1,0:T(8,128)(2,1)} %get-tuple-element.13.refs_0_, bf16[288,640]{1,0:T(8,128)(2,1)} %copy-done, bf16[288,640]{1,0:T(8,128)(2,1)} %copy-done.1, bf16[288,640]{1,0:T(8,128)(2,1)} %copy-done.2, ...), custom_call_target="tpu_custom_call" | custom-call | tf_op jit(solution)/shard_map/partial_acts/pallas_call | solution.py:83
  113.0 20.0 %all_to_all.25 = bf16[8,192,384]{2,1,0:T(8,128)(2,1)S(1)} all-to-all(bf16[8,192,384]{2,1,0:T(8,128)(2,1)} %partial_acts.1), channel_id=1, replica_groups=mesh['node'=32,'e'=4,'q'=4,'c'=2] {'q','c'}, dimensions={0} | all-to-all | bytes 2359296 | tf_op jit(solution)/shard_map/all_to_all | solution.py:19
  133.0 0.2 convert_reduce_fusion
  133.2 0.1 fusion.4
  133.2 12.2 %all-gather = bf16[384,384]{1,0:T(8,128)(2,1)S(1)} all-gather(bf16[96,384]{1,0:T(8,128)(2,1)S(1)} %fusion.4), channel_id=2, replica_groups=mesh['node'=32,'e'=4,'q'=4,'c'=2] {'q'}, dimensions={0}, use_global_device_ids=true | all-gather | bytes 368640 | tf_op jit(solution)/shard_map/all_gather | solution.py:188
  145.4 1.9 collective-permute-start.7
  147.3 1.5 collective-permute-done.7.other
  148.9 0.7 copy-done.7
  149.6 2.9 %down_rows.1 = bf16[384,640]{1,0:T(8,128)(2,1)} custom-call(s32[8]{0:T(128)} %broadcast_xor_fusion.order, bf16[4,96,384]{2,1,0:T(8,128)(2,1)} %bitcast.42, bf16[4,96,384]{2,1,0:T(8,128)(2,1)} %copy-done.7, bf16[288,640]{1,0:T(8,128)(2,1)} %get-tuple-element.13.refs_0_, bf16[288,640]{1,0:T(8,128)(2,1)} %copy-done, bf16[288,640]{1,0:T(8,128)(2,1)} %copy-done.1, ...), custom_call_target="tpu_custom_call" | custom-call | tf_op jit(solution)/shard_map/down_rows/pallas_call | solution.py:111
  152.5 1.9 reshape.82
  154.4 6.3 %all-to-all-start.3 = ((bf16[32,3,4,640]{3,2,1,0:T(4,128)(2,1)}), bf16[32,3,4,640]{3,2,1,0:T(4,128)(2,1)S(1)}, u32[]{:S(2)}, u32[]{:S(2)}) async-start(bf16[32,3,4,640]{3,2,1,0:T(4,128)(2,1)} %reshape.82), calls=%async_computation.3 | async-start | bytes 983040 | tf_op jit(solution)/shard_map/all_to_all | solution.py:19
  160.7 0.1 copy.51
  160.9 17.2 %all-to-all-done.3 = bf16[32,3,4,640]{3,2,1,0:T(4,128)(2,1)S(1)} async-done(((bf16[32,3,4,640]{3,2,1,0:T(4,128)(2,1)}), bf16[32,3,4,640]{3,2,1,0:T(4,128)(2,1)S(1)}, u32[]{:S(2)}, u32[]{:S(2)}) %all-to-all-start.3) | async-done | bytes 491552 | tf_op jit(solution)/shard_map/all_to_all | solution.py:19
  178.0 0.1 copy.53
  178.2 0.1 copy.58
  178.2 0.4 convolution_convert_fusion.1
  178.6 0.0 copy-start.8
  178.6 1.1 reshape.85
  179.7 4.6 %all-to-all-start.4 = ((bf16[32,2,5120]{2,1,0:T(2,128)(2,1)}), bf16[32,2,5120]{2,1,0:T(2,128)(2,1)S(1)}, u32[]{:S(2)}, u32[]{:S(2)}) async-start(bf16[32,2,5120]{2,1,0:T(2,128)(2,1)} %reshape.85), calls=%async_computation.4 | async-start | bytes 1310720 | tf_op jit(solution)/shard_map/all_to_all | solution.py:19
  184.2 0.1 reduce_sum.30
  184.3 0.1 copy.44
  184.4 0.1 fusion.8
  184.5 21.6 %all-to-all-done.4 = bf16[32,2,5120]{2,1,0:T(2,128)(2,1)S(1)} async-done(((bf16[32,2,5120]{2,1,0:T(2,128)(2,1)}), bf16[32,2,5120]{2,1,0:T(2,128)(2,1)S(1)}, u32[]{:S(2)}, u32[]{:S(2)}) %all-to-all-start.4) | async-done | bytes 655392 | tf_op jit(solution)/shard_map/all_to_all | solution.py:19
  206.2 0.2 reshape.86
  206.4 0.8 convolution_convert_fusion.3
  (37 shorter events, 0.2 us)
Async XLA Ops:
  5.0 45.4 %all-to-all-start = ((bf16[32,2,5124]{2,1,0:T(2,128)(2,1)}), bf16[32,2,5124]{2,1,0:T(2,128)(2,1)S(1)}, u32[]{:S(2)}, u32[]{:S(2)}) async-start(bf16[32,2,5124]{2,1,0:T(2,128)(2,1)} %reshape.76), calls=%async_computation | async-start | bytes 1343488 | tf_op jit(solution)/shard_map/all_to_all | solution.py:19
  51.7 9.8 %copy-start.9 = (s32[8]{0:T(128)S(1)}, s32[8]{0:T(128)}, u32[]{:S(2)}) copy-start(s32[8]{0:T(128)} %constant.30.clone) | copy-start | bytes 100
  52.7 40.7 %all-to-all-start.1 = ((bf16[32,3,4,640]{3,2,1,0:T(4,128)(2,1)}), bf16[32,3,4,640]{3,2,1,0:T(4,128)(2,1)S(1)}, u32[]{:S(2)}, u32[]{:S(2)}) async-start(bf16[32,3,4,640]{3,2,1,0:T(4,128)(2,1)} %bitcast.6), calls=%async_computation.1 | async-start | bytes 983040 | tf_op jit(solution)/shard_map/all_to_all | solution.py:19
  65.6 18.8 %collective-permute-start = (bf16[288,640]{1,0:T(8,128)(2,1)}, bf16[288,640]{1,0:T(8,128)(2,1)S(1)}, u32[]{:S(2)}, u32[]{:S(2)}) collective-permute-start(bf16[288,640]{1,0:T(8,128)(2,1)} %get-tuple-element.14), channel_id=1, source_target_pairs={{0,6},{1,7},{2,4},{3,5},{4,2},{5,3},{6,0},{7,1},{8,14},{9,15},{10,... | collective-permute-start | bytes 1105928 | tf_op jit(solution)/shard_map/ppermute | solution.py:145
  70.2 21.2 %collective-permute-start.1 = (bf16[288,640]{1,0:T(8,128)(2,1)}, bf16[288,640]{1,0:T(8,128)(2,1)S(1)}, u32[]{:S(2)}, u32[]{:S(2)}) collective-permute-start(bf16[288,640]{1,0:T(8,128)(2,1)} %get-tuple-element.15), channel_id=1, source_target_pairs={{0,4},{1,5},{2,6},{3,7},{4,0},{5,1},{6,2},{7,3},{8,12},{9,13},{10,... | collective-permute-start | bytes 1105928 | tf_op jit(solution)/shard_map/ppermute | solution.py:145
  72.7 21.6 %collective-permute-start.2 = (bf16[288,640]{1,0:T(8,128)(2,1)}, bf16[288,640]{1,0:T(8,128)(2,1)S(1)}, u32[]{:S(2)}, u32[]{:S(2)}) collective-permute-start(bf16[288,640]{1,0:T(8,128)(2,1)} %get-tuple-element.16), channel_id=1, source_target_pairs={{0,2},{1,3},{2,0},{3,1},{4,6},{5,7},{6,4},{7,5},{8,10},{9,11},{10,... | collective-permute-start | bytes 1105928 | tf_op jit(solution)/shard_map/ppermute | solution.py:145
  74.8 24.3 %collective-permute-start.3 = (bf16[288,640]{1,0:T(8,128)(2,1)}, bf16[288,640]{1,0:T(8,128)(2,1)S(1)}, u32[]{:S(2)}, u32[]{:S(2)}) collective-permute-start(bf16[288,640]{1,0:T(8,128)(2,1)} %get-tuple-element.17), channel_id=1, source_target_pairs={{0,7},{1,6},{2,5},{3,4},{4,3},{5,2},{6,1},{7,0},{8,15},{9,14},{10,... | collective-permute-start | bytes 1105928 | tf_op jit(solution)/shard_map/ppermute | solution.py:145
  78.3 27.8 %collective-permute-start.4 = (bf16[288,640]{1,0:T(8,128)(2,1)}, bf16[288,640]{1,0:T(8,128)(2,1)S(1)}, u32[]{:S(2)}, u32[]{:S(2)}) collective-permute-start(bf16[288,640]{1,0:T(8,128)(2,1)} %get-tuple-element.18), channel_id=1, source_target_pairs={{0,5},{1,4},{2,7},{3,6},{4,1},{5,0},{6,3},{7,2},{8,13},{9,12},{10,... | collective-permute-start | bytes 1105928 | tf_op jit(solution)/shard_map/ppermute | solution.py:145
  84.4 23.0 %copy-start = (bf16[288,640]{1,0:T(8,128)(2,1)}, bf16[288,640]{1,0:T(8,128)(2,1)S(1)}, u32[]{:S(2)}) copy-start(bf16[288,640]{1,0:T(8,128)(2,1)S(1)} %collective-permute-done.refs_1_) | copy-start | bytes 1105924
  84.4 23.0 %collective-permute-start.5 = (bf16[288,640]{1,0:T(8,128)(2,1)}, bf16[288,640]{1,0:T(8,128)(2,1)S(1)}, u32[]{:S(2)}, u32[]{:S(2)}) collective-permute-start(bf16[288,640]{1,0:T(8,128)(2,1)} %get-tuple-element.19), channel_id=1, source_target_pairs={{0,3},{1,2},{2,1},{3,0},{4,7},{5,6},{6,5},{7,4},{8,11},{9,10},{10,... | collective-permute-start | bytes 1105928 | tf_op jit(solution)/shard_map/ppermute | solution.py:145
  91.4 16.0 %copy-start.1 = (bf16[288,640]{1,0:T(8,128)(2,1)}, bf16[288,640]{1,0:T(8,128)(2,1)S(1)}, u32[]{:S(2)}) copy-start(bf16[288,640]{1,0:T(8,128)(2,1)S(1)} %collective-permute-done.1.refs_2_) | copy-start | bytes 1105924
  91.4 16.0 %collective-permute-start.6 = (bf16[288,640]{1,0:T(8,128)(2,1)}, bf16[288,640]{1,0:T(8,128)(2,1)}, u32[]{:S(2)}, u32[]{:S(2)}) collective-permute-start(bf16[288,640]{1,0:T(8,128)(2,1)} %get-tuple-element.20), channel_id=1, source_target_pairs={{0,1},{1,0},{2,3},{3,2},{4,5},{5,4},{6,7},{7,6},{8,9},{9,8},{10,11... | collective-permute-start | bytes 1105928 | tf_op jit(solution)/shard_map/ppermute | solution.py:145
  94.2 13.1 %copy-start.2 = (bf16[288,640]{1,0:T(8,128)(2,1)}, bf16[288,640]{1,0:T(8,128)(2,1)S(1)}, u32[]{:S(2)}) copy-start(bf16[288,640]{1,0:T(8,128)(2,1)S(1)} %collective-permute-done.2.refs_3_) | copy-start | bytes 1105924
  99.1 8.3 %copy-start.3 = (bf16[288,640]{1,0:T(8,128)(2,1)}, bf16[288,640]{1,0:T(8,128)(2,1)S(1)}, u32[]{:S(2)}) copy-start(bf16[288,640]{1,0:T(8,128)(2,1)S(1)} %collective-permute-done.3.refs_4_) | copy-start | bytes 1105924
  106.1 1.3 copy-start.4
  107.4 0.7 copy-start.5
  145.4 3.5 %copy-start.6 = (bf16[384,384]{1,0:T(8,128)(2,1)}, bf16[384,384]{1,0:T(8,128)(2,1)S(1)}, u32[]{:S(2)}) copy-start(bf16[384,384]{1,0:T(8,128)(2,1)S(1)} %all-gather) | copy-start | bytes 884740
  145.4 3.5 %collective-permute-start.7 = (bf16[4,96,384]{2,1,0:T(8,128)(2,1)S(1)}, bf16[4,96,384]{2,1,0:T(8,128)(2,1)S(1)}, u32[]{:S(2)}, u32[]{:S(2)}) collective-permute-start(bf16[4,96,384]{2,1,0:T(8,128)(2,1)S(1)} %bitcast.41), channel_id=1, source_target_pairs={{0,1},{1,0},{2,3},{3,2},{4,5},{5,4},{6,7},{7,6},{8,9},{9,8},{10,11... | collective-permute-start | bytes 884744 | tf_op jit(solution)/shard_map/ppermute | solution.py:189
  148.9 0.7 copy-start.7
  154.4 23.6 %all-to-all-start.3 = ((bf16[32,3,4,640]{3,2,1,0:T(4,128)(2,1)}), bf16[32,3,4,640]{3,2,1,0:T(4,128)(2,1)S(1)}, u32[]{:S(2)}, u32[]{:S(2)}) async-start(bf16[32,3,4,640]{3,2,1,0:T(4,128)(2,1)} %reshape.82), calls=%async_computation.3 | async-start | bytes 983040 | tf_op jit(solution)/shard_map/all_to_all | solution.py:19
  178.6 5.8 %copy-start.8 = (s32[4,3]{1,0:T(4,128)S(1)}, s32[4,3]{1,0:T(4,128)}, u32[]{:S(2)}) copy-start(s32[4,3]{1,0:T(4,128)} %param.9) | copy-start | bytes 148
  179.7 26.5 %all-to-all-start.4 = ((bf16[32,2,5120]{2,1,0:T(2,128)(2,1)}), bf16[32,2,5120]{2,1,0:T(2,128)(2,1)S(1)}, u32[]{:S(2)}, u32[]{:S(2)}) async-start(bf16[32,2,5120]{2,1,0:T(2,128)(2,1)} %reshape.85), calls=%async_computation.4 | async-start | bytes 1310720 | tf_op jit(solution)/shard_map/all_to_all | solution.py:19

commit v4 on v1

--- a/solution.py
+++ b/solution.py
@@ -9,6 +9,8 @@
 
 EXP_NODE = 4
 ALL = ("node", "e", "s")
+FIRST = (4, 5, 6, 7)
+THEN = (1, 2, 3)
 
 
 def swap(a, axis):
@@ -90,30 +92,24 @@
     )(order, rows, *blocks)
 
 
-def down_kernel(order, hidden, *refs):
+def order_kernel(order, *refs):
     blocks, out = refs[:-1], refs[-1]
-    weights = jnp.concatenate([block[...] for block in blocks], axis=0)
-    units = jnp.concatenate([hidden[order[k]] for k in range(len(blocks))], axis=0)
-    out[...] = lax.dot_general(
-        units, weights, (((0,), (0,)), ((), ())), preferred_element_type=jnp.float32
-    ).astype(jnp.bfloat16)
+    for k, block in enumerate(blocks):
+        out[order[k]] = block[...]
 
 
-def down_rows(order, hidden, blocks):
-    parts, size, all_rows = hidden.shape
-    width = blocks[0].shape[1]
+def ordered_down(order, blocks):
+    parts = len(blocks)
+    size, width = blocks[0].shape[0] // 3, blocks[0].shape[1]
     return pl.pallas_call(
-        down_kernel,
+        order_kernel,
         grid=(1,),
-        in_specs=[
-            pl.BlockSpec(memory_space=pltpu.SMEM),
-            pl.BlockSpec((parts, size, all_rows), lambda i: (0, 0, 0)),
-        ]
+        in_specs=[pl.BlockSpec(memory_space=pltpu.SMEM)]
         + [pl.BlockSpec((size, width), lambda i: (2, 0))] * parts,
-        out_specs=pl.BlockSpec((all_rows, width), lambda i: (0, 0)),
-        out_shape=jax.ShapeDtypeStruct((all_rows, width), jnp.bfloat16),
-        name="down_rows",
-    )(order, hidden, *blocks)
+        out_specs=pl.BlockSpec((parts, size, width), lambda i: (0, 0, 0)),
+        out_shape=jax.ShapeDtypeStruct((parts, size, width), jnp.bfloat16),
+        name="ordered_down",
+    )(order, *blocks)
 
 
 def on_device(tokens, node_pick, expert_pick, gate_weight, w_gate, w_up, w_down):
@@ -131,9 +127,10 @@
 
     order = jnp.arange(slices, dtype=jnp.int32) ^ lax.axis_index("s").astype(jnp.int32)
     cut = cut_weights(order, w_gate, w_up, w_down, slices)
-    blocks = [cut[0]]
-    for k in range(1, slices):
-        blocks.append(lax.ppermute(cut[k], "s", [(a, a ^ k) for a in range(slices)]))
+    blocks = list(cut)
+    for steps in (FIRST, THEN):
+        for k in steps:
+            blocks[k] = lax.ppermute(cut[k], "s", [(a, a ^ k) for a in range(slices)])
 
     dest_node = node_pick.reshape(slot_count)
     slot_order = jnp.arange(slot_count, dtype=jnp.int32)
@@ -143,7 +140,9 @@
     slot_rank = jnp.sum(earlier.astype(jnp.int32), axis=1)
     position = dest_node * node_cap + slot_rank
     place = jnp.arange(node_slots, dtype=jnp.int32)[:, None] == position[None, :]
-    home = jnp.sum(place.reshape(node_slots, tok_rows, 3).astype(jnp.bfloat16), axis=2)
+    by_token = place.reshape(node_slots, tok_rows, 3).astype(jnp.bfloat16)
+    home = lax.optimization_barrier(by_token[..., 0] + by_token[..., 1])
+    home = lax.optimization_barrier(home + by_token[..., 2])
     local_pick = expert_pick.reshape(tok_rows, 3, 2)
     weights = gate_weight.reshape(tok_rows, 3, 2).astype(jnp.float32)
     chosen = (local_pick[..., None] == jnp.arange(EXP_NODE, dtype=jnp.int32)).astype(jnp.float32)
@@ -171,11 +170,14 @@
     rows = arrived.reshape(all_rows, width)
 
     acts = partial_acts(order, rows, blocks)
+    down = ordered_down(order, blocks).reshape(slices * hidden_rows, width)
     acts = swap(acts, "s")
     acts = jnp.sum(acts.astype(jnp.float32), axis=0)
     hidden = (jax.nn.silu(acts[:hidden_rows]) * acts[hidden_rows:]).astype(jnp.bfloat16)
-    hidden = lax.all_gather(hidden, "s", axis=0)
-    made = down_rows(order, hidden, blocks)
+    hidden = lax.all_gather(hidden, "s", axis=0, tiled=True)
+    made = lax.dot_general(
+        hidden, down, (((0,), (0,)), ((), ())), preferred_element_type=jnp.float32
+    ).astype(jnp.bfloat16)
     returned = swap(made.reshape(dev_count, quads, 4, width), ("e", "s"))
     expert_out = returned.reshape(EXP_NODE, slices, slot_count, width).transpose(0, 2, 1, 3)
     expert_out = expert_out.reshape(EXP_NODE * slot_count, feature_dim)

time: 208 us -> 205 us (0.986)
  blocking collectives: 33.7 us -> 13 us
  waiting for transfers between devices: 86.1 us -> 99.6 us
  starting transfers between devices: 62.7 us -> 67.1 us
    all_to_all x1 -> x0, blocking collectives: 20 us -> none  [swap(): return lax.all_to_all(a, axis, split_axis=0, concat_axis=0, tiled=True)]
    all_to_all x4 -> x5, waiting for transfers between devices: 62.1 us -> 75.6 us  [swap(): return lax.all_to_all(a, axis, split_axis=0, concat_axis=0, tiled=True)]
    all_to_all x4 -> x5, starting transfers between devices: 42.7 us -> 47.1 us  [swap(): return lax.all_to_all(a, axis, split_axis=0, concat_axis=0, tiled=True)]
  transfers between devices with their start and end apart: 11 -> 12, of which waited for: 7 -> 8; matrix products, arithmetic and copies ran while one was open for 1% -> 1% of each run, Pallas kernels for 2% -> 3%
where the time goes in v4:
time: 205 us; the launch traced here: 204 us
  waiting for transfers between devices  99.6 us (49%)
  starting transfers between devices  67.1 us (33%)
  blocking collectives  13 us (6%)
  Pallas kernels  10.1 us (5%)
  local copies, waits for them, and re-layouts  9.84 us (5%)
  matrix products  2.43 us (1%)
    all_to_all x5, waiting for transfers between devices, swap(): return lax.all_to_all(a, axis, split_axis=0, concat_axis=0, tiled=True)  75.6 us
    all_to_all x5, starting transfers between devices, swap(): return lax.all_to_all(a, axis, split_axis=0, concat_axis=0, tiled=True)  47.1 us
    ppermute x7, waiting for transfers between devices, on_device(): blocks[k] = lax.ppermute(cut[k], 's', [(a, a ^ k) for a in range(slices)])  24 us
    ppermute x7, starting transfers between devices, on_device(): blocks[k] = lax.ppermute(cut[k], 's', [(a, a ^ k) for a in range(slices)])  20 us
    all_gather x1, blocking collectives, on_device(): hidden = lax.all_gather(hidden, 's', axis=0, tiled=True)  13 us
    pallas_call x1, Pallas kernels, partial_acts(): pl.pallas_call(act_kernel, grid=(1,), in_specs=[pl.BlockSpec(memory_space...  4.13 us
  transfers between devices with their start and end apart: 12, of which 8 were waited for; matrix products, arithmetic and copies ran while one was open for 1% of the time, Pallas kernels for 3%

profile of v4, /device:TPU:16, one launch (start us, length us, event | category | flops | bytes accessed | tf_op | source)
XLA Modules:
  0.0 203.8 jit_solution(16139931137137079018)
XLA Ops:
  0.0 0.8 eq.71
  0.8 0.2 convert_reduce_fusion.1
  1.0 0.8 copy.44
  1.7 0.8 copy.45
  2.5 0.1 select_reduce_fusion
  2.6 0.8 broadcast_in_dim.4
  3.5 0.1 reshape.78
  3.6 0.3 convolution_convert_fusion
  3.9 1.1 reshape.79
  5.0 22.0 %all-to-all-start = ((bf16[32,2,5124]{2,1,0:T(2,128)(2,1)}), bf16[32,2,5124]{2,1,0:T(2,128)(2,1)S(1)}, u32[]{:S(2)}, u32[]{:S(2)}) async-start(bf16[32,2,5124]{2,1,0:T(2,128)(2,1)} %reshape.79), calls=%async_computation | async-start | bytes 1343488 | tf_op jit(solution)/shard_map/all_to_all | solution.py:17
  27.0 0.1 eq.87
  27.1 23.3 %all-to-all-done = bf16[32,2,5124]{2,1,0:T(2,128)(2,1)S(1)} async-done(((bf16[32,2,5124]{2,1,0:T(2,128)(2,1)}), bf16[32,2,5124]{2,1,0:T(2,128)(2,1)S(1)}, u32[]{:S(2)}, u32[]{:S(2)}) %all-to-all-start) | async-done | bytes 655904 | tf_op jit(solution)/shard_map/all_to_all | solution.py:17
  50.4 0.5 reshape.80
  50.9 0.1 reduce_window_sum.11
  51.0 0.1 copy.49
  51.1 0.1 copy.48
  51.3 0.1 compare_and_fusion
  51.3 0.3 convolution_convert_fusion.2
  51.6 0.1 copy.56
  51.7 1.0 copy.51
  52.6 8.8 %all-to-all-start.1 = ((bf16[32,3,4,640]{3,2,1,0:T(4,128)(2,1)}), bf16[32,3,4,640]{3,2,1,0:T(4,128)(2,1)S(1)}, u32[]{:S(2)}, u32[]{:S(2)}) async-start(bf16[32,3,4,640]{3,2,1,0:T(4,128)(2,1)} %bitcast.6), calls=%async_computation.1 | async-start | bytes 983040 | tf_op jit(solution)/shard_map/all_to_all | solution.py:17
  61.4 0.5 iota_xor_fusion.order
  61.9 3.6 %cut_weights.1 = (bf16[288,640]{1,0:T(8,128)(2,1)}, bf16[288,640]{1,0:T(8,128)(2,1)}, bf16[288,640]{1,0:T(8,128)(2,1)}, bf16[288,640]{1,0:T(8,128)(2,1)}, bf16[2...) custom-call(s32[8]{0:T(128)} %iota_xor_fusion.order, ...), custom_call_target="tpu_custom_call" | custom-call | tf_op jit(solution)/shard_map/cut_weights/pallas_call | solution.py:52
  65.6 2.2 %collective-permute-start = (bf16[288,640]{1,0:T(8,128)(2,1)}, bf16[288,640]{1,0:T(8,128)(2,1)S(1)}, u32[]{:S(2)}, u32[]{:S(2)}) collective-permute-start(bf16[288,640]{1,0:T(8,128)(2,1)} %get-tuple-element.14), channel_id=1, source_target_pairs={{0,1},{1,0},{2,3},{3,2},{4,5},{5,4},{6,7},{7,6},{8,9},{9,8},{10,11... | collective-permute-start | bytes 1105928 | tf_op jit(solution)/shard_map/ppermute | solution.py:133
  67.7 3.5 %collective-permute-start.1 = (bf16[288,640]{1,0:T(8,128)(2,1)}, bf16[288,640]{1,0:T(8,128)(2,1)S(1)}, u32[]{:S(2)}, u32[]{:S(2)}) collective-permute-start(bf16[288,640]{1,0:T(8,128)(2,1)} %get-tuple-element.15), channel_id=1, source_target_pairs={{0,2},{1,3},{2,0},{3,1},{4,6},{5,7},{6,4},{7,5},{8,10},{9,11},{10,... | collective-permute-start | bytes 1105928 | tf_op jit(solution)/shard_map/ppermute | solution.py:133
  71.3 1.9 collective-permute-start.2
  73.2 3.6 %collective-permute-start.3 = (bf16[288,640]{1,0:T(8,128)(2,1)}, bf16[288,640]{1,0:T(8,128)(2,1)S(1)}, u32[]{:S(2)}, u32[]{:S(2)}) collective-permute-start(bf16[288,640]{1,0:T(8,128)(2,1)} %get-tuple-element.17), channel_id=1, source_target_pairs={{0,4},{1,5},{2,6},{3,7},{4,0},{5,1},{6,2},{7,3},{8,12},{9,13},{10,... | collective-permute-start | bytes 1105928 | tf_op jit(solution)/shard_map/ppermute | solution.py:133
  76.9 2.0 collective-permute-start.4
  78.9 0.0 collective-permute-done.refs_1_
  78.9 0.0 copy-start
  78.9 4.4 %collective-permute-start.5 = (bf16[288,640]{1,0:T(8,128)(2,1)}, bf16[288,640]{1,0:T(8,128)(2,1)}, u32[]{:S(2)}, u32[]{:S(2)}) collective-permute-start(bf16[288,640]{1,0:T(8,128)(2,1)} %get-tuple-element.19), channel_id=1, source_target_pairs={{0,6},{1,7},{2,4},{3,5},{4,2},{5,3},{6,0},{7,1},{8,14},{9,15},{10,... | collective-permute-start | bytes 1105928 | tf_op jit(solution)/shard_map/ppermute | solution.py:133
  83.4 0.0 collective-permute-done.1.refs_2_
  83.4 2.3 %collective-permute-start.6 = (bf16[288,640]{1,0:T(8,128)(2,1)}, bf16[288,640]{1,0:T(8,128)(2,1)}, u32[]{:S(2)}, u32[]{:S(2)}) collective-permute-start(bf16[288,640]{1,0:T(8,128)(2,1)} %get-tuple-element.20), channel_id=1, source_target_pairs={{0,7},{1,6},{2,5},{3,4},{4,3},{5,2},{6,1},{7,0},{8,15},{9,14},{10,... | collective-permute-start | bytes 1105928 | tf_op jit(solution)/shard_map/ppermute | solution.py:133
  85.7 0.0 all-to-all-done.1
  85.7 0.9 reshape.84.rows
  86.6 3.7 %collective-permute-done.2.refs_3_ = bf16[288,640]{1,0:T(8,128)(2,1)S(1)} collective-permute-done((bf16[288,640]{1,0:T(8,128)(2,1)}, bf16[288,640]{1,0:T(8,128)(2,1)S(1)}, u32[]{:S(2)}, u32[]{:S(2)}) %collective-permute-start.2) | collective-permute-done | bytes 368672 | tf_op jit(solution)/shard_map/ppermute | solution.py:133
  90.3 0.0 collective-permute-done.3.refs_4_
  90.3 3.7 %collective-permute-done.4.refs_5_ = bf16[288,640]{1,0:T(8,128)(2,1)S(1)} collective-permute-done((bf16[288,640]{1,0:T(8,128)(2,1)}, bf16[288,640]{1,0:T(8,128)(2,1)S(1)}, u32[]{:S(2)}, u32[]{:S(2)}) %collective-permute-start.4) | collective-permute-done | bytes 368672 | tf_op jit(solution)/shard_map/ppermute | solution.py:133
  94.0 9.8 %collective-permute-done.5.refs_6_ = bf16[288,640]{1,0:T(8,128)(2,1)} collective-permute-done((bf16[288,640]{1,0:T(8,128)(2,1)}, bf16[288,640]{1,0:T(8,128)(2,1)}, u32[]{:S(2)}, u32[]{:S(2)}) %collective-permute-start.5) | collective-permute-done | bytes 368672 | tf_op jit(solution)/shard_map/ppermute | solution.py:133
  103.9 6.8 %collective-permute-done.6.refs_7_ = bf16[288,640]{1,0:T(8,128)(2,1)} collective-permute-done((bf16[288,640]{1,0:T(8,128)(2,1)}, bf16[288,640]{1,0:T(8,128)(2,1)}, u32[]{:S(2)}, u32[]{:S(2)}) %collective-permute-start.6) | collective-permute-done | bytes 368672 | tf_op jit(solution)/shard_map/ppermute | solution.py:133
  110.6 4.1 %partial_acts.1 = bf16[8,192,384]{2,1,0:T(8,128)(2,1)} custom-call(s32[8]{0:T(128)} %iota_xor_fusion.order, bf16[384,640]{1,0:T(8,128)(2,1)} %reshape.84.rows, bf16[288,640]{1,0:T(8,128)(2,1)} %get-tuple-element.13.refs_0_, bf16[288,640]{1,0:T(8,128)(2,1)} %copy-done, bf16[288,640]{1,0:T(8,128)(2,1)} %copy-done.1, bf16[288,640]{1,0:T(8,128)(2,1)} %copy-done.2, ...), custom_call_target="tpu_custom_call" | custom-call | tf_op jit(solution)/shard_map/partial_acts/pallas_call | solution.py:81
  114.8 3.6 %all-to-all-start.2 = ((bf16[8,192,384]{2,1,0:T(8,128)(2,1)}), bf16[8,192,384]{2,1,0:T(8,128)(2,1)S(1)}, u32[]{:S(2)}, u32[]{:S(2)}) async-start(bf16[8,192,384]{2,1,0:T(8,128)(2,1)} %partial_acts.1), calls=%async_computation.2 | async-start | bytes 2359296 | tf_op jit(solution)/shard_map/all_to_all | solution.py:17
  118.3 2.3 %ordered_down.1 = bf16[8,96,640]{2,1,0:T(8,128)(2,1)} custom-call(s32[8]{0:T(128)} %iota_xor_fusion.order, bf16[288,640]{1,0:T(8,128)(2,1)} %get-tuple-element.13.refs_0_, bf16[288,640]{1,0:T(8,128)(2,1)} %copy-done, bf16[288,640]{1,0:T(8,128)(2,1)} %copy-done.1, bf16[288,640]{1,0:T(8,128)(2,1)} %copy-done.2, bf16[288,640]{1,0:T(8,128)(2,1)} %copy-done.3, ...), custom_call_target="tpu_custom_call" | custom-call | tf_op jit(solution)/shard_map/ordered_down/pallas_call | solution.py:104
  120.7 13.5 %all-to-all-done.2 = bf16[8,192,384]{2,1,0:T(8,128)(2,1)S(1)} async-done(((bf16[8,192,384]{2,1,0:T(8,128)(2,1)}), bf16[8,192,384]{2,1,0:T(8,128)(2,1)S(1)}, u32[]{:S(2)}, u32[]{:S(2)}) %all-to-all-start.2) | async-done | bytes 1179680 | tf_op jit(solution)/shard_map/all_to_all | solution.py:17
  134.1 0.2 convert_reduce_fusion
  134.3 0.1 fusion.4
  134.4 13.0 %all_gather.3 = bf16[768,384]{1,0:T(8,128)(2,1)S(1)} all-gather(bf16[96,384]{1,0:T(8,128)(2,1)S(1)} %fusion.4), channel_id=1, replica_groups=mesh['node'=32,'e'=4,'s'=8] {'s'}, dimensions={0}, use_global_device_ids=true | all-gather | bytes 663552 | tf_op jit(solution)/shard_map/all_gather | solution.py:177
  147.4 0.7 convolution_convert_fusion.4
  148.1 0.9 reshape.86
  149.0 8.2 %all-to-all-start.3 = ((bf16[32,3,4,640]{3,2,1,0:T(4,128)(2,1)}), bf16[32,3,4,640]{3,2,1,0:T(4,128)(2,1)S(1)}, u32[]{:S(2)}, u32[]{:S(2)}) async-start(bf16[32,3,4,640]{3,2,1,0:T(4,128)(2,1)} %reshape.86), calls=%async_computation.3 | async-start | bytes 983040 | tf_op jit(solution)/shard_map/all_to_all | solution.py:17
  157.3 0.1 copy.50
  157.4 17.2 %all-to-all-done.3 = bf16[32,3,4,640]{3,2,1,0:T(4,128)(2,1)S(1)} async-done(((bf16[32,3,4,640]{3,2,1,0:T(4,128)(2,1)}), bf16[32,3,4,640]{3,2,1,0:T(4,128)(2,1)S(1)}, u32[]{:S(2)}, u32[]{:S(2)}) %all-to-all-start.3) | async-done | bytes 491552 | tf_op jit(solution)/shard_map/all_to_all | solution.py:17
  174.6 0.1 copy.52
  174.7 0.1 copy.57
  174.7 0.4 convolution_convert_fusion.1
  175.1 0.0 copy-start.6
  175.1 1.1 reshape.89
  176.2 4.6 %all-to-all-start.4 = ((bf16[32,2,5120]{2,1,0:T(2,128)(2,1)}), bf16[32,2,5120]{2,1,0:T(2,128)(2,1)S(1)}, u32[]{:S(2)}, u32[]{:S(2)}) async-start(bf16[32,2,5120]{2,1,0:T(2,128)(2,1)} %reshape.89), calls=%async_computation.4 | async-start | bytes 1310720 | tf_op jit(solution)/shard_map/all_to_all | solution.py:17
  180.8 0.1 reduce_sum.30
  180.9 0.1 copy.43
  181.0 0.1 fusion.8
  181.0 21.6 %all-to-all-done.4 = bf16[32,2,5120]{2,1,0:T(2,128)(2,1)S(1)} async-done(((bf16[32,2,5120]{2,1,0:T(2,128)(2,1)}), bf16[32,2,5120]{2,1,0:T(2,128)(2,1)S(1)}, u32[]{:S(2)}, u32[]{:S(2)}) %all-to-all-start.4) | async-done | bytes 655392 | tf_op jit(solution)/shard_map/all_to_all | solution.py:17
  202.7 0.2 reshape.90
  202.9 0.8 convolution_convert_fusion.3
  (31 shorter events, 0.2 us)
Async XLA Ops:
  5.0 45.4 %all-to-all-start = ((bf16[32,2,5124]{2,1,0:T(2,128)(2,1)}), bf16[32,2,5124]{2,1,0:T(2,128)(2,1)S(1)}, u32[]{:S(2)}, u32[]{:S(2)}) async-start(bf16[32,2,5124]{2,1,0:T(2,128)(2,1)} %reshape.79), calls=%async_computation | async-start | bytes 1343488 | tf_op jit(solution)/shard_map/all_to_all | solution.py:17
  52.6 33.0 %all-to-all-start.1 = ((bf16[32,3,4,640]{3,2,1,0:T(4,128)(2,1)}), bf16[32,3,4,640]{3,2,1,0:T(4,128)(2,1)S(1)}, u32[]{:S(2)}, u32[]{:S(2)}) async-start(bf16[32,3,4,640]{3,2,1,0:T(4,128)(2,1)} %bitcast.6), calls=%async_computation.1 | async-start | bytes 983040 | tf_op jit(solution)/shard_map/all_to_all | solution.py:17
  65.6 13.3 %collective-permute-start = (bf16[288,640]{1,0:T(8,128)(2,1)}, bf16[288,640]{1,0:T(8,128)(2,1)S(1)}, u32[]{:S(2)}, u32[]{:S(2)}) collective-permute-start(bf16[288,640]{1,0:T(8,128)(2,1)} %get-tuple-element.14), channel_id=1, source_target_pairs={{0,1},{1,0},{2,3},{3,2},{4,5},{5,4},{6,7},{7,6},{8,9},{9,8},{10,11... | collective-permute-start | bytes 1105928 | tf_op jit(solution)/shard_map/ppermute | solution.py:133
  67.7 15.6 %collective-permute-start.1 = (bf16[288,640]{1,0:T(8,128)(2,1)}, bf16[288,640]{1,0:T(8,128)(2,1)S(1)}, u32[]{:S(2)}, u32[]{:S(2)}) collective-permute-start(bf16[288,640]{1,0:T(8,128)(2,1)} %get-tuple-element.15), channel_id=1, source_target_pairs={{0,2},{1,3},{2,0},{3,1},{4,6},{5,7},{6,4},{7,5},{8,10},{9,11},{10,... | collective-permute-start | bytes 1105928 | tf_op jit(solution)/shard_map/ppermute | solution.py:133
  71.3 19.0 %collective-permute-start.2 = (bf16[288,640]{1,0:T(8,128)(2,1)}, bf16[288,640]{1,0:T(8,128)(2,1)S(1)}, u32[]{:S(2)}, u32[]{:S(2)}) collective-permute-start(bf16[288,640]{1,0:T(8,128)(2,1)} %get-tuple-element.16), channel_id=1, source_target_pairs={{0,3},{1,2},{2,1},{3,0},{4,7},{5,6},{6,5},{7,4},{8,11},{9,10},{10,... | collective-permute-start | bytes 1105928 | tf_op jit(solution)/shard_map/ppermute | solution.py:133
  73.2 17.1 %collective-permute-start.3 = (bf16[288,640]{1,0:T(8,128)(2,1)}, bf16[288,640]{1,0:T(8,128)(2,1)S(1)}, u32[]{:S(2)}, u32[]{:S(2)}) collective-permute-start(bf16[288,640]{1,0:T(8,128)(2,1)} %get-tuple-element.17), channel_id=1, source_target_pairs={{0,4},{1,5},{2,6},{3,7},{4,0},{5,1},{6,2},{7,3},{8,12},{9,13},{10,... | collective-permute-start | bytes 1105928 | tf_op jit(solution)/shard_map/ppermute | solution.py:133
  76.9 17.2 %collective-permute-start.4 = (bf16[288,640]{1,0:T(8,128)(2,1)}, bf16[288,640]{1,0:T(8,128)(2,1)S(1)}, u32[]{:S(2)}, u32[]{:S(2)}) collective-permute-start(bf16[288,640]{1,0:T(8,128)(2,1)} %get-tuple-element.18), channel_id=1, source_target_pairs={{0,5},{1,4},{2,7},{3,6},{4,1},{5,0},{6,3},{7,2},{8,13},{9,12},{10,... | collective-permute-start | bytes 1105928 | tf_op jit(solution)/shard_map/ppermute | solution.py:133
  78.9 31.7 %copy-start = (bf16[288,640]{1,0:T(8,128)(2,1)}, bf16[288,640]{1,0:T(8,128)(2,1)S(1)}, u32[]{:S(2)}) copy-start(bf16[288,640]{1,0:T(8,128)(2,1)S(1)} %collective-permute-done.refs_1_) | copy-start | bytes 1105924
  78.9 24.9 %collective-permute-start.5 = (bf16[288,640]{1,0:T(8,128)(2,1)}, bf16[288,640]{1,0:T(8,128)(2,1)}, u32[]{:S(2)}, u32[]{:S(2)}) collective-permute-start(bf16[288,640]{1,0:T(8,128)(2,1)} %get-tuple-element.19), channel_id=1, source_target_pairs={{0,6},{1,7},{2,4},{3,5},{4,2},{5,3},{6,0},{7,1},{8,14},{9,15},{10,... | collective-permute-start | bytes 1105928 | tf_op jit(solution)/shard_map/ppermute | solution.py:133
  83.4 27.2 %copy-start.1 = (bf16[288,640]{1,0:T(8,128)(2,1)}, bf16[288,640]{1,0:T(8,128)(2,1)S(1)}, u32[]{:S(2)}) copy-start(bf16[288,640]{1,0:T(8,128)(2,1)S(1)} %collective-permute-done.1.refs_2_) | copy-start | bytes 1105924
  83.4 27.2 %collective-permute-start.6 = (bf16[288,640]{1,0:T(8,128)(2,1)}, bf16[288,640]{1,0:T(8,128)(2,1)}, u32[]{:S(2)}, u32[]{:S(2)}) collective-permute-start(bf16[288,640]{1,0:T(8,128)(2,1)} %get-tuple-element.20), channel_id=1, source_target_pairs={{0,7},{1,6},{2,5},{3,4},{4,3},{5,2},{6,1},{7,0},{8,15},{9,14},{10,... | collective-permute-start | bytes 1105928 | tf_op jit(solution)/shard_map/ppermute | solution.py:133
  90.3 20.3 %copy-start.2 = (bf16[288,640]{1,0:T(8,128)(2,1)}, bf16[288,640]{1,0:T(8,128)(2,1)S(1)}, u32[]{:S(2)}) copy-start(bf16[288,640]{1,0:T(8,128)(2,1)S(1)} %collective-permute-done.2.refs_3_) | copy-start | bytes 1105924
  90.3 20.3 %copy-start.3 = (bf16[288,640]{1,0:T(8,128)(2,1)}, bf16[288,640]{1,0:T(8,128)(2,1)S(1)}, u32[]{:S(2)}) copy-start(bf16[288,640]{1,0:T(8,128)(2,1)S(1)} %collective-permute-done.3.refs_4_) | copy-start | bytes 1105924
  94.0 16.6 %copy-start.4 = (bf16[288,640]{1,0:T(8,128)(2,1)}, bf16[288,640]{1,0:T(8,128)(2,1)S(1)}, u32[]{:S(2)}) copy-start(bf16[288,640]{1,0:T(8,128)(2,1)S(1)} %collective-permute-done.4.refs_5_) | copy-start | bytes 1105924
  114.8 19.4 %all-to-all-start.2 = ((bf16[8,192,384]{2,1,0:T(8,128)(2,1)}), bf16[8,192,384]{2,1,0:T(8,128)(2,1)S(1)}, u32[]{:S(2)}, u32[]{:S(2)}) async-start(bf16[8,192,384]{2,1,0:T(8,128)(2,1)} %partial_acts.1), calls=%async_computation.2 | async-start | bytes 2359296 | tf_op jit(solution)/shard_map/all_to_all | solution.py:17
  120.7 26.7 %copy-start.5 = (bf16[8,96,640]{2,1,0:T(8,128)(2,1)S(1)}, bf16[8,96,640]{2,1,0:T(8,128)(2,1)}, u32[]{:S(2)}) copy-start(bf16[8,96,640]{2,1,0:T(8,128)(2,1)} %ordered_down.1) | copy-start | bytes 2949124
  149.0 25.6 %all-to-all-start.3 = ((bf16[32,3,4,640]{3,2,1,0:T(4,128)(2,1)}), bf16[32,3,4,640]{3,2,1,0:T(4,128)(2,1)S(1)}, u32[]{:S(2)}, u32[]{:S(2)}) async-start(bf16[32,3,4,640]{3,2,1,0:T(4,128)(2,1)} %reshape.86), calls=%async_computation.3 | async-start | bytes 983040 | tf_op jit(solution)/shard_map/all_to_all | solution.py:17
  175.1 5.8 %copy-start.6 = (s32[4,3]{1,0:T(4,128)S(1)}, s32[4,3]{1,0:T(4,128)}, u32[]{:S(2)}) copy-start(s32[4,3]{1,0:T(4,128)} %param.8) | copy-start | bytes 148
  176.2 26.5 %all-to-all-start.4 = ((bf16[32,2,5120]{2,1,0:T(2,128)(2,1)}), bf16[32,2,5120]{2,1,0:T(2,128)(2,1)S(1)}, u32[]{:S(2)}, u32[]{:S(2)}) async-start(bf16[32,2,5120]{2,1,0:T(2,128)(2,1)} %reshape.89), calls=%async_computation.4 | async-start | bytes 1310720 | tf_op jit(solution)/shard_map/all_to_all | solution.py:17
